TPU v7x, 32 devices: a whole 2x2x4 slice. The times are simulated.
32 devices in a mesh: pool: 4 (over z), fft: 8 (over y, x, core).
Axes of the slice: x: 2, y: 2, z: 4, core: 2. Of those that a mesh axis runs over, the one named last changes fastest.
Arguments:
- orbitals: bfloat16 [4, 2, 1, 160, 25600], P('pool', None, None, 'fft'), may hold values from -6 to 6
- stick_map: int32 [16000], replicated, may hold values from -1 to 25599, as said below
- kpoint_grid: int32 [4, 3], replicated, may hold values from 0 to 3, as said below
Outputs:
- exchange_action: bfloat16 [4, 2, 1, 160, 25600], P('pool', None, None, 'fft')
Inputs may be any that keep to these rules, and one draw needn't show every extreme that they name: `stick_map`: entries other than -1 are distinct columns. Slots come in blocks of 2000 per index of fft; in each block at least half of the slots are live, and in every draw some block has all 2000 live. `kpoint_grid`: rows are distinct.
All inputs are finite; a program needn't handle non-finite values.
Results may differ from a plain program's by a relative error of at most 0.011.
Values may be sent and summed in bfloat16 or wider, within the bound.
No kernel may reach another device: no remote copies, remote signals or barrier semaphores. Data moves between devices by JAX's collectives and lax.ppermute only.
A program may use at most 64 MiB of HBM per device.

v0:
```python
import math

import jax
import jax.numpy as jnp
from jax import lax
from jax.sharding import PartitionSpec as P

NG = 160
KMESH = 4


SPACING_BOHR = 0.1875
SCREENING = 0.106


def shifted(value, axis, steps):
    count = lax.axis_size(axis)
    pairs = [(source, (source + steps) % count) for source in range(count)]
    return lax.ppermute(value, axis, pairs)


def dft_table(grid_size, orientation):
    positions = jnp.arange(grid_size, dtype=jnp.int32)
    product = positions[:, None] * positions[None, :] % grid_size
    angle = product.astype(jnp.float32) * (2.0 * math.pi / grid_size)
    cosine = jnp.cos(angle)
    sine = orientation * jnp.sin(angle)
    upper = jnp.stack([cosine, sine], axis=1)
    lower = jnp.stack([-sine, cosine], axis=1)
    return jnp.stack([upper, lower], axis=0).astype(jnp.bfloat16)


def signed(frequency, grid_size):
    return jnp.where(frequency >= grid_size // 2, frequency - grid_size, frequency)


def kernel_table(columns, shift_q, grid_size):
    live_slot = columns >= 0
    column_ids = jnp.where(live_slot, columns, 0)
    freq_x = signed(column_ids % grid_size, grid_size)
    freq_y = signed(column_ids // grid_size, grid_size)
    freq_z = signed(jnp.arange(grid_size, dtype=jnp.int32), grid_size)
    radius = grid_size // 2
    inside = (freq_x * freq_x + freq_y * freq_y)[None, :] + (freq_z * freq_z)[
        :, None
    ] <= radius * radius
    inside = jnp.logical_and(inside, live_slot[None, :])
    wave_x = freq_x.astype(jnp.float32) + shift_q[0]
    wave_y = freq_y.astype(jnp.float32) + shift_q[1]
    wave_z = freq_z.astype(jnp.float32) + shift_q[2]
    square = (wave_z * wave_z)[:, None] + (wave_x * wave_x + wave_y * wave_y)[None, :]
    cell = SPACING_BOHR * grid_size
    exponent = math.pi * math.pi * square / (cell * cell * SCREENING * SCREENING)
    weights = cell * cell / math.pi * -jnp.expm1(-exponent) / square / float(grid_size) ** 3
    return jnp.where(inside, weights, 0.0)


def momentum(kpoint_grid, pool_rank, pool_count):
    pool_rows = jnp.arange(pool_count, dtype=jnp.int32)
    earlier = (pool_rank + pool_count - 1) % pool_count
    current = jnp.sum(jnp.where((pool_rows == pool_rank)[:, None], kpoint_grid, 0), axis=0)
    previous = jnp.sum(jnp.where((pool_rows == earlier)[:, None], kpoint_grid, 0), axis=0)
    return (current - previous).astype(jnp.float32) / KMESH


def pair_density(own_bands, received):
    band_count = own_bands.shape[1]
    real_own = own_bands[0].astype(jnp.float32)[:, None]
    imag_own = own_bands[1].astype(jnp.float32)[:, None]
    real_recv = received[0].astype(jnp.float32)[None]
    imag_recv = received[1].astype(jnp.float32)[None]
    real_part = real_recv * real_own + imag_recv * imag_own
    imag_part = real_recv * imag_own - imag_recv * real_own
    stacked = jnp.stack([real_part, imag_part], axis=2)
    return stacked.reshape((band_count * band_count, 2) + own_bands.shape[2:]).astype(jnp.bfloat16)


def action_of(received, field):
    band_count = received.shape[1]
    field = field.reshape((band_count, band_count) + field.shape[1:])
    real_recv = received[0].astype(jnp.float32)[None]
    imag_recv = received[1].astype(jnp.float32)[None]
    real_field = field[:, :, 0]
    imag_field = field[:, :, 1]
    real_part = -jnp.sum(real_recv * real_field - imag_recv * imag_field, axis=1)
    imag_part = -jnp.sum(real_recv * imag_field + imag_recv * real_field, axis=1)
    return jnp.stack([real_part, imag_part], axis=0).astype(jnp.bfloat16)


def apply_table(data, table, form):
    return jnp.einsum(form, data, table, preferred_element_type=jnp.float32)


def column_pass(picked, weights, forward, backward):
    spectrum = apply_table(picked, forward, "pczs,czdk->pdks")
    scaled = (spectrum * weights).astype(jnp.bfloat16)
    return apply_table(scaled, backward, "pczs,czdk->pdks").astype(jnp.bfloat16)


def local(orbitals, stick_map, kpoint_grid):
    grid_size = NG
    moved = shifted(orbitals, "pool", 1)
    own_bands = orbitals[0].reshape(orbitals.shape[1:4] + (grid_size, grid_size))
    received = moved[0].reshape(orbitals.shape[1:4] + (grid_size, grid_size))
    fft_count = lax.axis_size("fft")
    fft_rank = lax.axis_index("fft")
    pool_count = lax.axis_size("pool")
    pool_rank = lax.axis_index("pool")
    shift_q = momentum(kpoint_grid, pool_rank, pool_count)
    forward = dft_table(grid_size, -1.0)
    backward = dft_table(grid_size, 1.0)
    column_share = grid_size * grid_size // fft_count
    share_ids = fft_rank * column_share + jnp.arange(column_share, dtype=jnp.int32)
    ordered_map = jnp.sort(stick_map)
    found_at = jnp.searchsorted(ordered_map, share_ids)
    found_at = jnp.minimum(found_at, stick_map.shape[0] - 1)
    own_present = jnp.take(ordered_map, found_at) == share_ids
    weights = kernel_table(jnp.where(own_present, share_ids, -1), shift_q, grid_size)

    def potential(pair_block):
        along_x = apply_table(pair_block, forward, "pczyx,cxek->pezyk").astype(jnp.bfloat16)
        along_y = apply_table(along_x, forward, "pczyx,cyek->pezkx").astype(jnp.bfloat16)
        piece_block = lax.all_to_all(along_y, "fft", split_axis=3, concat_axis=2, tiled=True)
        flat_piece = piece_block.reshape(piece_block.shape[:3] + (column_share,))
        scaled_back = column_pass(flat_piece, weights, forward, backward).reshape(piece_block.shape)
        spectrum = lax.all_to_all(scaled_back, "fft", split_axis=2, concat_axis=3, tiled=True)
        back_y = apply_table(spectrum, backward, "pczkx,ckey->pezyx").astype(jnp.bfloat16)
        return apply_table(back_y, backward, "pczyk,ckex->pezyx")

    density = pair_density(own_bands, received)
    field = lax.map(lambda single_pair: potential(single_pair[None])[0], density)
    result = action_of(received, field)
    return result.reshape((1,) + result.shape[:3] + (grid_size * grid_size,))


def solution(mesh):
    return jax.shard_map(
        local,
        mesh=mesh,
        in_specs=(P("pool", None, None, "fft", None), P(), P()),
        out_specs=P("pool", None, None, "fft", None),
        check_vma=False,
    )
```

profile of v0, /device:TPU:0, one launch (start us, length us, event | category | flops | bytes accessed | tf_op | source)
XLA Modules:
  0.0 470.6 jit_solution(1656870052998849744)
XLA Ops:
  3.1 8.6 %sort.15 = (s32[16000]{0:T(1024)S(1)}, s32[16000]{0:T(1024)}) sort(s32[16000]{0:T(1024)} %param.6, s32[16000]{0:T(1024)S(1)} %iota.64), dimensions={0}, to_apply=%region_0.1 | sort | flops 224000 | bytes 256000 | tf_op jit(solution)/shard_map/jit(sort)/sort | solution.py:114
  11.7 238.8 %while.28 = (s32[]{:T(128)}, u32[3200]{0:T(1024)S(1)}, u32[3200]{0:T(1024)S(1)}, s32[16000]{0:T(1024)S(1)}, s32[]{:T(128)}, /*index=5*/s32[]{:T(128)}, s32[]{:T(128)}, s32[]{}) while((s32[]{:T(128)}, u32[3200]{0:T(1024)S(1)}, u32[3200]{0:T(1024)S(1)}, s32[16000]{0:T(1024)S(1)}, s32[]{:T(128)}, /*index=5*/s32[]{:T(128)}, s32[]{:T(128)}, ...), condition=%wide.region_2.3_spmd.clone, body=%wide.region_1.2_spmd.clone.sunk | while | flops 64900 | bytes 227697 | solution.py:115
  11.9 16.9 %gather_fusion = s32[3200]{0:T(1024)S(1)} fusion(s32[16000]{0:T(1024)S(1)} %get-tuple-element.202, u32[4096]{0:T(1024)S(1)} %pad_clamp_fusion.3), kind=kCustom, calls=%fused_computation.clone.clone.1 | custom fusion | bytes 38400 | tf_op jit(solution)/shard_map/jit(searchsorted)/jit(_searchsorted_scan_impl)/vmap(jit(_searchsorted_scan_impl))/while/body/eval_jaxpr/gather | solution.py:115
  28.9 16.9 %gather_fusion = s32[3200]{0:T(1024)S(1)} fusion(s32[16000]{0:T(1024)S(1)} %get-tuple-element.202, u32[4096]{0:T(1024)S(1)} %pad_clamp_fusion.3), kind=kCustom, calls=%fused_computation.clone.clone.1 | custom fusion | bytes 38400 | tf_op jit(solution)/shard_map/jit(searchsorted)/jit(_searchsorted_scan_impl)/vmap(jit(_searchsorted_scan_impl))/while/body/eval_jaxpr/gather | solution.py:115
  46.0 16.9 %gather_fusion = s32[3200]{0:T(1024)S(1)} fusion(s32[16000]{0:T(1024)S(1)} %get-tuple-element.202, u32[4096]{0:T(1024)S(1)} %pad_clamp_fusion.3), kind=kCustom, calls=%fused_computation.clone.clone.1 | custom fusion | bytes 38400 | tf_op jit(solution)/shard_map/jit(searchsorted)/jit(_searchsorted_scan_impl)/vmap(jit(_searchsorted_scan_impl))/while/body/eval_jaxpr/gather | solution.py:115
  63.0 16.9 %gather_fusion = s32[3200]{0:T(1024)S(1)} fusion(s32[16000]{0:T(1024)S(1)} %get-tuple-element.202, u32[4096]{0:T(1024)S(1)} %pad_clamp_fusion.3), kind=kCustom, calls=%fused_computation.clone.clone.1 | custom fusion | bytes 38400 | tf_op jit(solution)/shard_map/jit(searchsorted)/jit(_searchsorted_scan_impl)/vmap(jit(_searchsorted_scan_impl))/while/body/eval_jaxpr/gather | solution.py:115
  80.0 16.9 %gather_fusion = s32[3200]{0:T(1024)S(1)} fusion(s32[16000]{0:T(1024)S(1)} %get-tuple-element.202, u32[4096]{0:T(1024)S(1)} %pad_clamp_fusion.3), kind=kCustom, calls=%fused_computation.clone.clone.1 | custom fusion | bytes 38400 | tf_op jit(solution)/shard_map/jit(searchsorted)/jit(_searchsorted_scan_impl)/vmap(jit(_searchsorted_scan_impl))/while/body/eval_jaxpr/gather | solution.py:115
  97.1 16.9 %gather_fusion = s32[3200]{0:T(1024)S(1)} fusion(s32[16000]{0:T(1024)S(1)} %get-tuple-element.202, u32[4096]{0:T(1024)S(1)} %pad_clamp_fusion.3), kind=kCustom, calls=%fused_computation.clone.clone.1 | custom fusion | bytes 38400 | tf_op jit(solution)/shard_map/jit(searchsorted)/jit(_searchsorted_scan_impl)/vmap(jit(_searchsorted_scan_impl))/while/body/eval_jaxpr/gather | solution.py:115
  114.1 16.9 %gather_fusion = s32[3200]{0:T(1024)S(1)} fusion(s32[16000]{0:T(1024)S(1)} %get-tuple-element.202, u32[4096]{0:T(1024)S(1)} %pad_clamp_fusion.3), kind=kCustom, calls=%fused_computation.clone.clone.1 | custom fusion | bytes 38400 | tf_op jit(solution)/shard_map/jit(searchsorted)/jit(_searchsorted_scan_impl)/vmap(jit(_searchsorted_scan_impl))/while/body/eval_jaxpr/gather | solution.py:115
  131.2 16.9 %gather_fusion = s32[3200]{0:T(1024)S(1)} fusion(s32[16000]{0:T(1024)S(1)} %get-tuple-element.202, u32[4096]{0:T(1024)S(1)} %pad_clamp_fusion.3), kind=kCustom, calls=%fused_computation.clone.clone.1 | custom fusion | bytes 38400 | tf_op jit(solution)/shard_map/jit(searchsorted)/jit(_searchsorted_scan_impl)/vmap(jit(_searchsorted_scan_impl))/while/body/eval_jaxpr/gather | solution.py:115
  148.2 16.9 %gather_fusion = s32[3200]{0:T(1024)S(1)} fusion(s32[16000]{0:T(1024)S(1)} %get-tuple-element.202, u32[4096]{0:T(1024)S(1)} %pad_clamp_fusion.3), kind=kCustom, calls=%fused_computation.clone.clone.1 | custom fusion | bytes 38400 | tf_op jit(solution)/shard_map/jit(searchsorted)/jit(_searchsorted_scan_impl)/vmap(jit(_searchsorted_scan_impl))/while/body/eval_jaxpr/gather | solution.py:115
  165.3 16.9 %gather_fusion = s32[3200]{0:T(1024)S(1)} fusion(s32[16000]{0:T(1024)S(1)} %get-tuple-element.202, u32[4096]{0:T(1024)S(1)} %pad_clamp_fusion.3), kind=kCustom, calls=%fused_computation.clone.clone.1 | custom fusion | bytes 38400 | tf_op jit(solution)/shard_map/jit(searchsorted)/jit(_searchsorted_scan_impl)/vmap(jit(_searchsorted_scan_impl))/while/body/eval_jaxpr/gather | solution.py:115
  182.3 16.9 %gather_fusion = s32[3200]{0:T(1024)S(1)} fusion(s32[16000]{0:T(1024)S(1)} %get-tuple-element.202, u32[4096]{0:T(1024)S(1)} %pad_clamp_fusion.3), kind=kCustom, calls=%fused_computation.clone.clone.1 | custom fusion | bytes 38400 | tf_op jit(solution)/shard_map/jit(searchsorted)/jit(_searchsorted_scan_impl)/vmap(jit(_searchsorted_scan_impl))/while/body/eval_jaxpr/gather | solution.py:115
  199.4 16.9 %gather_fusion = s32[3200]{0:T(1024)S(1)} fusion(s32[16000]{0:T(1024)S(1)} %get-tuple-element.202, u32[4096]{0:T(1024)S(1)} %pad_clamp_fusion.3), kind=kCustom, calls=%fused_computation.clone.clone.1 | custom fusion | bytes 38400 | tf_op jit(solution)/shard_map/jit(searchsorted)/jit(_searchsorted_scan_impl)/vmap(jit(_searchsorted_scan_impl))/while/body/eval_jaxpr/gather | solution.py:115
  216.4 16.9 %gather_fusion = s32[3200]{0:T(1024)S(1)} fusion(s32[16000]{0:T(1024)S(1)} %get-tuple-element.202, u32[4096]{0:T(1024)S(1)} %pad_clamp_fusion.3), kind=kCustom, calls=%fused_computation.clone.clone.1 | custom fusion | bytes 38400 | tf_op jit(solution)/shard_map/jit(searchsorted)/jit(_searchsorted_scan_impl)/vmap(jit(_searchsorted_scan_impl))/while/body/eval_jaxpr/gather | solution.py:115
  233.4 16.9 %gather_fusion = s32[3200]{0:T(1024)S(1)} fusion(s32[16000]{0:T(1024)S(1)} %get-tuple-element.202, u32[4096]{0:T(1024)S(1)} %pad_clamp_fusion.3), kind=kCustom, calls=%fused_computation.clone.clone.1 | custom fusion | bytes 38400 | tf_op jit(solution)/shard_map/jit(searchsorted)/jit(_searchsorted_scan_impl)/vmap(jit(_searchsorted_scan_impl))/while/body/eval_jaxpr/gather | solution.py:115
  254.1 19.3 %fusion.44 = (bf16[20,25600]{1,0:T(8,128)(2,1)}, bf16[20,25600]{1,0:T(8,128)(2,1)S(1)}) fusion(bf16[1,2,1,20,25600]{4,1,3,2,0:T(2,128)(2,1)} %param.5, bf16[1,2,1,20,25600]{4,1,3,2,0:T(2,128)(2,1)S(1)} %collective-permute-done), kind=kLoop, calls=%fused_computation.59 | loop fusion | flops 6144000 | bytes 6144000 | tf_op jit(solution)/shard_map/convert.5
  280.9 7.6 %fusion.10 = bf16[1,2,20,160,160]{4,3,2,1,0:T(8,128)(2,1)} fusion(bf16[1,1,1,20,160,160]{5,4,2,3,1,0:T(8,128)(2,1)} %bitcast.197, bf16[1,1,1,20,160,160]{5,4,2,3,1,0:T(8,128)(2,1)} %bitcast.196, bf16[1,160,2,160]{1,3,0,2:T(8,128)(2,1)} %get-tuple-element.136, bf16[1,160,2,160]{1,3,0,2:T(8,128)(2,1)} %get-tuple-element.137), kind=kOutput, calls=%fused_computation.21 | convolution fusion | flops 1317683200 | bytes 4300800 | tf_op jit(solution)/shard_map/while/body/eval_jaxpr/pczyx,cyek->pezkx/dot_general | solution.py:91
  300.2 16.9 %gather_fusion.1 = s32[3200]{0:T(1024)S(1)} fusion(s32[16000]{0:T(1024)S(1)} %get-tuple-element.207, s32[4096]{0:T(1024)S(1)} %pad_clamp_fusion.1), kind=kCustom, calls=%fused_computation.1 | custom fusion | bytes 38400 | tf_op jit(solution)/shard_map/jit(_take)/gather | solution.py:117
  321.8 17.6 %all-to-all-done = bf16[1,2,20,160,160]{4,1,2,0,3:T(2,128)(2,1)} async-done(((bf16[1,2,20,160,160]{4,1,2,0,3:T(2,128)(2,1)}), bf16[1,2,20,160,160]{4,1,2,0,3:T(2,128)(2,1)}, u32[]{:S(2)}, u32[]{:S(2)}) %all-to-all-start) | async-done | bytes 2048032 | tf_op jit(solution)/shard_map/while/body/eval_jaxpr/all_to_all | solution.py:123
  359.6 7.5 %reshape.548 = bf16[1,2,160,20,160]{4,3,2,1,0:T(8,128)(2,1)} reshape(bf16[2,160,3200]{2,1,0:T(8,128)(2,1)} %fusion.4) | data formatting | bytes 4096000 | tf_op jit(solution)/shard_map/while/body/eval_jaxpr/reshape | solution.py:125
  374.3 41.8 %all_to_all.38 = bf16[1,2,160,20,160]{4,1,3,0,2:T(2,128)(2,1)S(1)} all-to-all(bf16[1,2,160,20,160]{4,1,3,0,2:T(2,128)(2,1)S(1)} %copy.60), channel_id=1, replica_groups=mesh['pool'=4,'fft'=8] {'fft'}, dimensions={2} | all-to-all | bytes 4096000 | tf_op jit(solution)/shard_map/while/body/eval_jaxpr/all_to_all | solution.py:126
  448.5 9.1 %negate_convert_fusion.1 = (bf16[1,1,1,20,25600]{4,2,3,1,0:T(2,128)(2,1)S(1)}, bf16[1,1,1,20,25600]{4,2,3,1,0:T(2,128)(2,1)}) fusion(f32[1,1,1,20,25600]{4,2,3,1,0:T(1,128)} %squeeze.35, f32[1,1,1,20,25600]{4,2,3,1,0:T(1,128)} %squeeze.34, bf16[1,2,1,20,25600]{4,1,3,2,0:T(2,128)(2,1)S(1)} %collective-permute-done), kind=kLoop, calls=%fused_computation.56 | loop fusion | flops 6144000 | bytes 8192000 | tf_op jit(solution)/shard_map/convert
  457.6 8.3 %pad_maximum_fusion = bf16[1,2,1,20,25600]{4,2,3,1,0:T(2,128)(2,1)S(1)} fusion(bf16[1,1,1,20,25600]{4,2,3,1,0:T(2,128)(2,1)} %get-tuple-element.134, bf16[1,1,1,20,25600]{4,2,3,1,0:T(2,128)(2,1)S(1)} %get-tuple-element.133), kind=kLoop, calls=%fused_computation.17 | loop fusion | flops 1024000 | bytes 4096000 | tf_op jit(solution)/shard_map/stack | solution.py:87
  (117 shorter events, 95.2 us)
Async XLA Ops:
  0.0 254.1 %collective-permute-start = (bf16[1,2,1,20,25600]{4,1,3,2,0:T(2,128)(2,1)}, bf16[1,2,1,20,25600]{4,1,3,2,0:T(2,128)(2,1)S(1)}, u32[]{:S(2)}, u32[]{:S(2)}) collective-permute-start(bf16[1,2,1,20,25600]{4,1,3,2,0:T(2,128)(2,1)} %param.5), channel_id=1, source_target_pairs={{0,8},{8,16},{16,24},{24,0},{1,9},{9,17},{17,25},{25,1},{2,10},{10... | collective-permute-start | bytes 6144008 | tf_op jit(solution)/shard_map/ppermute | solution.py:19
  11.7 238.8 %copy-start.3 = (s32[4,3]{1,0:T(4,128)S(1)}, s32[4,3]{1,0:T(4,128)}, u32[]{:S(2)}) copy-start(s32[4,3]{1,0:T(4,128)} %param.7) | copy-start | bytes 148
  295.4 44.0 %all-to-all-start = ((bf16[1,2,20,160,160]{4,1,2,0,3:T(2,128)(2,1)}), bf16[1,2,20,160,160]{4,1,2,0,3:T(2,128)(2,1)}, u32[]{:S(2)}, u32[]{:S(2)}) async-start(bf16[1,2,20,160,160]{4,1,2,0,3:T(2,128)(2,1)} %copy.57), calls=%async_computation | async-start | bytes 6553600 | tf_op jit(solution)/shard_map/while/body/eval_jaxpr/all_to_all | solution.py:123
  347.1 6.6 %copy-start = (bf16[1,160,2,160]{1,3,2,0:T(8,128)(2,1)S(1)}, bf16[1,160,2,160]{1,3,2,0:T(8,128)(2,1)}, u32[]{:S(2)}) copy-start(bf16[1,160,2,160]{1,3,2,0:T(8,128)(2,1)} %get-tuple-element.138) | copy-start | bytes 307204
  347.1 6.6 %copy-start.1 = (bf16[1,160,2,160]{1,3,0,2:T(8,128)(2,1)S(1)}, bf16[1,160,2,160]{1,3,0,2:T(8,128)(2,1)}, u32[]{:S(2)}) copy-start(bf16[1,160,2,160]{1,3,0,2:T(8,128)(2,1)} %get-tuple-element.136) | copy-start | bytes 307204
  347.1 6.6 %copy-start.2 = (bf16[1,160,2,160]{1,3,0,2:T(8,128)(2,1)S(1)}, bf16[1,160,2,160]{1,3,0,2:T(8,128)(2,1)}, u32[]{:S(2)}) copy-start(bf16[1,160,2,160]{1,3,0,2:T(8,128)(2,1)} %get-tuple-element.137) | copy-start | bytes 307204
where the time goes:
time: 476 us; the launch traced here: 471 us
  local copies, waits for them, and re-layouts  331 us (70%)
  other arithmetic  53.5 us (11%)
  blocking collectives  41.8 us (9%)
  waiting for transfers between devices  17.6 us (4%)
  matrix products  17.3 us (4%)
  starting transfers between devices  7.76 us (2%)
    gather x14, local copies, waits for them, and re-layouts, local(): found_at = jnp.searchsorted(ordered_map, share_ids)  237 us
    all_to_all x1, blocking collectives, potential(): lax.all_to_all(scaled_back, 'fft', split_axis=2, concat_axis=3, tiled=True)  41.8 us
    another operation x5, other arithmetic  30.4 us
    all_to_all x1, waiting for transfers between devices, potential(): lax.all_to_all(along_y, 'fft', split_axis=3, concat_axis=2, tiled=True)  17.6 us
    dot_general x4, matrix products, apply_table(): return jnp.einsum(form, data, table, preferred_element_type=jnp.float32)  17.3 us
    gather x1, local copies, waits for them, and re-layouts, local(): own_present = jnp.take(ordered_map, found_at) == share_ids  16.9 us
    reshape x2, local copies, waits for them, and re-layouts, potential(): column_pass(flat_piece, weights, forward, backward)  14.7 us
  transfers between devices with their start and end apart: 2, of which 1 were waited for; matrix products, arithmetic and copies ran while one was open for 58% of the time, Pallas kernels for 0%

commit v1 on v0

v1 whole, which is shorter than its diff:
```python
import functools
import math

import jax
import jax.numpy as jnp
import numpy as np
from jax import lax
from jax.experimental import pallas as pl
from jax.experimental.pallas import tpu as pltpu
from jax.sharding import PartitionSpec as P

NG = 160
KMESH = 4
LANES = 128


SPACING_BOHR = 0.1875
SCREENING = 0.106

GROUP = math.lcm(NG, LANES) // NG
TILES = GROUP * NG // LANES
GROUPS = NG // GROUP
ROWS = 2 * NG * NG // LANES
STEP = 2 * TILES
OUTER = NG - LANES
HALF = LANES // 2


def shifted(value, axis, steps):
    count = lax.axis_size(axis)
    pairs = [(source, (source + steps) % count) for source in range(count)]
    return lax.ppermute(value, axis, pairs)


def dft_table(grid_size, orientation):
    positions = np.arange(grid_size)
    angle = (positions[:, None] * positions[None, :] % grid_size) * (2.0 * np.pi / grid_size)
    cosine = np.cos(angle)
    sine = orientation * np.sin(angle)
    upper = np.stack([cosine, sine], axis=1)
    lower = np.stack([-sine, cosine], axis=1)
    return np.stack([upper, lower], axis=0)


def inner(table, axis):
    size = table.shape[axis]
    return np.concatenate(
        [np.take(table, range(HALF), axis), np.take(table, range(size - HALF, size), axis)], axis
    )


def outer(table, axis):
    return np.take(table, range(HALF, table.shape[axis] - HALF), axis)


def padded(table, axis, size):
    widths = [(0, 0)] * table.ndim
    widths[axis] = (0, size - table.shape[axis])
    return np.pad(table, widths)


def tables(fft_count):
    share = NG // fft_count
    fwd = dft_table(NG, -1.0)
    bwd = dft_table(NG, 1.0)
    full = 2 * NG
    x_fwd = np.concatenate(
        [inner(fwd, 3).reshape(2, NG, 2 * LANES), padded(outer(fwd, 3), 3, LANES).reshape(2, NG, 2 * LANES)], 2
    )
    x_bwd = np.concatenate(
        [inner(bwd, 1).reshape(2 * LANES, 2, NG), padded(outer(bwd, 1), 1, LANES).reshape(2 * LANES, 2, NG)], 0
    )
    split = fwd.reshape(2, GROUPS, GROUP, 2, fft_count, share)
    y_fwd = split.transpose(4, 3, 5, 0, 2, 1).reshape(full, full)
    y_fwd_side = inner(fwd.reshape(2, GROUPS, GROUP, 2, NG).transpose(0, 2, 1, 3, 4), 4).reshape(full, 2 * LANES)
    z_fwd = fwd.transpose(2, 3, 0, 1).reshape(full, full)
    z_bwd = bwd.reshape(2, NG, 2, fft_count, share).transpose(3, 2, 4, 0, 1).reshape(full, full)
    order = bwd.reshape(2, NG, 2, GROUPS, GROUP).transpose(2, 4, 3, 0, 1)
    y_bwd = order.reshape(full, full)
    y_bwd_side = inner(order, 4).reshape(full, 2 * LANES)
    cast = lambda t: jnp.asarray(t.astype(np.float32).astype(jnp.bfloat16))
    return [cast(t) for t in (x_fwd, x_bwd, y_fwd, y_fwd_side, z_fwd, z_bwd, y_bwd, y_bwd_side)]


def signed(frequency, grid_size):
    return jnp.where(frequency >= grid_size // 2, frequency - grid_size, frequency)


def kernel_table(column_x, column_y, live, shift_q, grid_size):
    freq_x = signed(column_x, grid_size)
    freq_y = signed(column_y, grid_size)
    freq_z = signed(jnp.arange(grid_size, dtype=jnp.int32), grid_size)
    radius = grid_size // 2
    inside = (freq_x * freq_x + freq_y * freq_y)[None, :] + (freq_z * freq_z)[:, None] <= radius * radius
    inside = jnp.logical_and(inside, live[None, :])
    wave_x = freq_x.astype(jnp.float32) + shift_q[0]
    wave_y = freq_y.astype(jnp.float32) + shift_q[1]
    wave_z = freq_z.astype(jnp.float32) + shift_q[2]
    square = (wave_z * wave_z)[:, None] + (wave_x * wave_x + wave_y * wave_y)[None, :]
    cell = SPACING_BOHR * grid_size
    exponent = math.pi * math.pi * square / (cell * cell * SCREENING * SCREENING)
    weights = cell * cell / math.pi * -jnp.expm1(-exponent) / square / float(grid_size) ** 3
    return jnp.where(inside, weights, 0.0)


def momentum(kpoint_grid, pool_rank, pool_count):
    pool_rows = jnp.arange(pool_count, dtype=jnp.int32)
    earlier = (pool_rank + pool_count - 1) % pool_count
    current = jnp.sum(jnp.where((pool_rows == pool_rank)[:, None], kpoint_grid, 0), axis=0)
    previous = jnp.sum(jnp.where((pool_rows == earlier)[:, None], kpoint_grid, 0), axis=0)
    return (current - previous).astype(jnp.float32) / KMESH


def one_hot(values, wanted):
    return (wanted[:, None] == values[None, :]).astype(jnp.bfloat16)


def column_weights(stick_map, kpoint_grid, fft_rank, share, side_share):
    pool_count = lax.axis_size("pool")
    shift_q = momentum(kpoint_grid, lax.axis_index("pool"), pool_count)
    lanes = jnp.arange(LANES, dtype=jnp.int32)
    inner_freq = jnp.where(lanes < HALF, lanes, lanes + OUTER)
    own_y = fft_rank * share + jnp.arange(share, dtype=jnp.int32)
    own_x = HALF + fft_rank * side_share + jnp.arange(side_share, dtype=jnp.int32)
    column_y = jnp.where(stick_map >= 0, stick_map // NG, -1)
    column_x = jnp.where(stick_map >= 0, stick_map % NG, -1)
    form = (((1,), (1,)), ((), ()))
    main = lax.dot_general(
        one_hot(column_y, own_y), one_hot(column_x, inner_freq), form, preferred_element_type=jnp.float32
    )
    side = lax.dot_general(
        one_hot(column_x, own_x), one_hot(column_y, inner_freq), form, preferred_element_type=jnp.float32
    )
    live = jnp.concatenate([main, side], axis=0).reshape(-1) > 0.5
    place = jnp.arange((share + side_share) * LANES, dtype=jnp.int32)
    row = place // LANES
    lane_freq = jnp.where(place % LANES < HALF, place % LANES, place % LANES + OUTER)
    is_main = row < share
    ids_x = jnp.where(is_main, lane_freq, HALF + fft_rank * side_share + row - share)
    ids_y = jnp.where(is_main, fft_rank * share + row, lane_freq)
    return kernel_table(ids_x, ids_y, live, shift_q, NG)


def dot(left, right, form=(((1,), (0,)), ((), ()))):
    return lax.dot_general(left, right, form, preferred_element_type=jnp.float32)


def pieces(ref, plane, tile, part):
    return ref[pl.ds(plane * ROWS + 2 * tile + part, GROUPS, stride=STEP), :]


def pairs_of(count):
    return [tuple(range(i, min(i + 2, count))) for i in range(0, count, 2)]


def forward_kernel(own_ref, recv_ref, x_ref, y_ref, side_ref, out_ref, own_f, recv_f, *, planes, fft_count):
    share = NG // fft_count
    side_share = OUTER // fft_count
    own_f[...] = own_ref[...].astype(jnp.float32)
    recv_f[...] = recv_ref[...].astype(jnp.float32)
    density = []
    for tile in range(TILES):
        real, imag = [], []
        for z in range(planes):
            ro, io = pieces(own_f, z, tile, 0), pieces(own_f, z, tile, 1)
            rr, ir = pieces(recv_f, z, tile, 0), pieces(recv_f, z, tile, 1)
            real.append(rr * ro + ir * io)
            imag.append(rr * io - ir * ro)
        density.append(
            (jnp.concatenate(real, 0).astype(jnp.bfloat16), jnp.concatenate(imag, 0).astype(jnp.bfloat16))
        )
    along_x = []
    for r in range(GROUP):
        left = jnp.concatenate([density[r][0], density[r + 1][0], density[r][1], density[r + 1][1]], axis=1)
        along_x.append(dot(left, x_ref[r]))

    def block(z, r, column):
        return along_x[r][z * GROUPS : (z + 1) * GROUPS, column * LANES : (column + 1) * LANES]

    def stacked(z, first):
        return jnp.concatenate([block(z, r, first + c) for c in range(2) for r in range(GROUP)], axis=0)

    for pair in pairs_of(planes):
        right = jnp.concatenate([stacked(z, 0) for z in pair], axis=1).astype(jnp.bfloat16)
        along_y = dot(y_ref[...], right)
        for n, z in enumerate(pair):
            for k in range(fft_count):
                out_ref[k, z, : 2 * share, :] = along_y[
                    2 * share * k : 2 * share * (k + 1), n * LANES : (n + 1) * LANES
                ].astype(jnp.bfloat16)
    side = stacked(0, 2)
    for z in range(1, planes):
        side = side + pltpu.roll(stacked(z, 2), z * OUTER, 1)
    side = side[:, : planes * OUTER].astype(jnp.bfloat16)
    side_y = dot(side, side_ref[...], (((0,), (0,)), ((), ())))
    for z in range(planes):
        for k in range(fft_count):
            row = z * OUTER + k * side_share
            out_ref[k, z, 2 * share :, :] = jnp.concatenate(
                [side_y[row : row + side_share, c * LANES : (c + 1) * LANES] for c in range(2)], axis=0
            ).astype(jnp.bfloat16)


def column_kernel(in_ref, weight_ref, fwd_ref, bwd_ref, out_ref, wide, *, fft_count):
    share = NG // fft_count
    side_share = OUTER // fft_count
    height = 2 * (share + side_share)
    wide[...] = in_ref[...].reshape(NG * height, LANES).astype(jnp.float32)

    def column(i):
        first = i if i < share else 2 * share + i - share
        jump = share if i < share else side_share
        return jnp.concatenate([wide[pl.ds(first + c * jump, NG, stride=height), :] for c in range(2)], axis=0)

    for pair in pairs_of(share + side_share):
        right = jnp.concatenate([column(i) for i in pair], axis=1).astype(jnp.bfloat16)
        spectrum = dot(fwd_ref[...], right)
        weight = weight_ref[:, pair[0] * LANES : (pair[-1] + 1) * LANES]
        scaled = jnp.concatenate([spectrum[:NG] * weight, spectrum[NG:] * weight], axis=0).astype(jnp.bfloat16)
        back = dot(bwd_ref[...], scaled)
        for n, i in enumerate(pair):
            for k in range(fft_count):
                out_ref[k, i, :, :] = back[
                    2 * share * k : 2 * share * (k + 1), n * LANES : (n + 1) * LANES
                ].astype(jnp.bfloat16)


def backward_kernel(
    in_ref, recv_ref, x_ref, y_ref, side_ref, out_ref, main_f, side_f, recv_f, out_f, *, planes, fft_count
):
    share = NG // fft_count
    side_share = OUTER // fft_count
    height = 2 * share

    @pl.when(pl.program_id(0) == 0)
    def _():
        for k in range(fft_count):
            main_f[pl.ds(k * share * height, share * height), :] = (
                in_ref[k, :share].reshape(share * height, LANES).astype(jnp.float32)
            )
            side_f[pl.ds(k * side_share * height, side_share * height), :] = (
                in_ref[k, share:].reshape(side_share * height, LANES).astype(jnp.float32)
            )

    recv_f[...] = recv_ref[...].astype(jnp.float32)
    base = pl.program_id(0) * planes

    def main_of(z):
        return jnp.concatenate(
            [main_f[pl.ds(base + z + c * share, NG, stride=height), :] for c in range(2)], axis=0
        )

    def side_of(z):
        return jnp.concatenate(
            [side_f[pl.ds(base + z + c * share, OUTER, stride=height), :] for c in range(2)], axis=1
        )

    back_y = []
    for pair in pairs_of(planes):
        right = jnp.concatenate([main_of(z) for z in pair], axis=1).astype(jnp.bfloat16)
        both = dot(y_ref[...], right)
        back_y += [both[:, n * LANES : (n + 1) * LANES] for n in range(len(pair))]
    packed = jnp.concatenate([side_of(z) for z in range(planes)], axis=0).astype(jnp.bfloat16)
    back_side = dot(side_ref[...], packed, (((1,), (1,)), ((), ())))
    if planes * OUTER < LANES:
        back_side = jnp.concatenate(
            [back_side, jnp.zeros((2 * NG, LANES - planes * OUTER), jnp.float32)], axis=1
        )
    turned = [back_side] + [pltpu.roll(back_side, LANES - z * OUTER, 1) for z in range(1, planes)]
    field = []
    for r in range(GROUP):
        rows = []
        for z in range(planes):
            parts = [v[c * NG + r * GROUPS : c * NG + (r + 1) * GROUPS] for v in (back_y[z], turned[z]) for c in range(2)]
            rows.append(jnp.concatenate(parts, axis=1))
        field.append(dot(jnp.concatenate(rows, axis=0).astype(jnp.bfloat16), x_ref[r]))
    for tile in range(TILES):
        values = []
        for c in range(2):
            value = None
            if tile < GROUP:
                value = field[tile][:, 2 * c * LANES : (2 * c + 1) * LANES]
            if tile > 0:
                late = field[tile - 1][:, (2 * c + 1) * LANES : (2 * c + 2) * LANES]
                value = late if value is None else value + late
            values.append(value)
        for z in range(planes):
            re, im = (v[z * GROUPS : (z + 1) * GROUPS] for v in values)
            rr, ir = pieces(recv_f, z, tile, 0), pieces(recv_f, z, tile, 1)
            out_f[pl.ds(z * ROWS + 2 * tile, GROUPS, stride=STEP), :] = ir * im - rr * re
            out_f[pl.ds(z * ROWS + 2 * tile + 1, GROUPS, stride=STEP), :] = -(rr * im + ir * re)
    out_ref[...] = out_f[...].astype(jnp.bfloat16)


def rows_of(orbitals):
    planes = orbitals.shape[3]
    split = orbitals.reshape(2, planes, NG * NG // LANES, LANES)
    return split.transpose(1, 2, 0, 3).reshape(planes * ROWS, LANES)


def whole(shape):
    return pl.BlockSpec(shape, lambda *_: (0,) * len(shape))


def x_windows(table, axis):
    placed = []
    for r in range(GROUP):
        first = r * (NG - LANES)
        widths = [(0, 0)] * table.ndim
        widths[axis] = (first, 2 * LANES - NG - first)
        placed.append(jnp.pad(table, widths).reshape(4 * LANES, 4 * LANES))
    return jnp.stack(placed)


def local(orbitals, stick_map, kpoint_grid):
    moved = shifted(orbitals, "pool", 1)
    planes_all = orbitals.shape[3]
    planes = GROUP if planes_all % GROUP == 0 else 1
    steps = planes_all // planes
    fft_count = lax.axis_size("fft")
    fft_rank = lax.axis_index("fft")
    share = NG // fft_count
    side_share = OUTER // fft_count
    columns = share + side_share
    x_fwd, x_bwd, y_fwd, y_fwd_side, z_fwd, z_bwd, y_bwd, y_bwd_side = tables(fft_count)
    x_fwd = x_windows(x_fwd, 1)
    x_bwd = x_windows(x_bwd, 2)
    weights = column_weights(stick_map, kpoint_grid, fft_rank, share, side_share)
    own = rows_of(orbitals)
    received = rows_of(moved)
    block = planes * ROWS
    row_spec = pl.BlockSpec((block, LANES), lambda s: (s, 0))
    params = pltpu.CompilerParams(vmem_limit_bytes=48 << 20)
    wide = lambda count: pltpu.VMEM((count, LANES), jnp.float32)
    spectrum = pl.pallas_call(
        functools.partial(forward_kernel, planes=planes, fft_count=fft_count),
        grid=(steps,),
        in_specs=[row_spec, row_spec, whole(x_fwd.shape), whole(y_fwd.shape), whole(y_fwd_side.shape)],
        out_specs=pl.BlockSpec((fft_count, planes, 2 * columns, LANES), lambda s: (0, s, 0, 0)),
        out_shape=jax.ShapeDtypeStruct((fft_count, planes_all, 2 * columns, LANES), jnp.bfloat16),
        scratch_shapes=[wide(block), wide(block)],
        compiler_params=params,
        name="density_xy",
    )(own, received, x_fwd, y_fwd, y_fwd_side)
    spectrum = lax.all_to_all(spectrum, "fft", 0, 0, tiled=True)
    scaled = pl.pallas_call(
        functools.partial(column_kernel, fft_count=fft_count),
        out_shape=jax.ShapeDtypeStruct((fft_count, columns, 2 * share, LANES), jnp.bfloat16),
        scratch_shapes=[wide(NG * 2 * columns)],
        compiler_params=params,
        name="columns",
    )(spectrum, weights, z_fwd, z_bwd)
    scaled = lax.all_to_all(scaled, "fft", 0, 0, tiled=True)
    result = pl.pallas_call(
        functools.partial(backward_kernel, planes=planes, fft_count=fft_count),
        grid=(steps,),
        in_specs=[whole(scaled.shape), row_spec, whole(x_bwd.shape), whole(y_bwd.shape), whole(y_bwd_side.shape)],
        out_specs=row_spec,
        out_shape=jax.ShapeDtypeStruct((planes_all * ROWS, LANES), jnp.bfloat16),
        scratch_shapes=[wide(NG * 2 * share), wide(OUTER * 2 * share), wide(block), wide(block)],
        compiler_params=params,
        name="yx_action",
    )(scaled, received, x_bwd, y_bwd, y_bwd_side)
    result = result.reshape(planes_all, NG * NG // LANES, 2, LANES).transpose(2, 0, 1, 3)
    return result.reshape(orbitals.shape)


def solution(mesh):
    return jax.shard_map(
        local,
        mesh=mesh,
        in_specs=(P("pool", None, None, "fft", None), P(), P()),
        out_specs=P("pool", None, None, "fft", None),
        check_vma=False,
    )
```

time: 476 us -> 132 us (0.28)
  local copies, waits for them, and re-layouts: 331 us -> 6.69 us
  other arithmetic: 53.5 us -> 6.53 us
  waiting for transfers between devices: 17.6 us -> 61.8 us
  Pallas kernels: 0 us -> 18.5 us
  matrix products: 17.3 us -> 2.95 us
  blocking collectives: 41.8 us -> 27.7 us
    gather x15 -> x0, local copies, waits for them, and re-layouts: 254 us -> none  [the longest x14 237 us: local(): found_at = jnp.searchsorted(ordered_map, share_ids)]
    ppermute x1, waiting for transfers between devices: 0.01 us -> 44.2 us  [shifted(): return lax.ppermute(value, axis, pairs)]
    another operation x7 -> x0, other arithmetic: 39.6 us -> none
    pallas_call x0 -> x3, Pallas kernels: none -> 18.5 us  [the longest x1 7.29 us: local(): pl.pallas_call(functools.partial(backward_kernel, planes=planes, fft_coun...]
    reshape x2 -> x0, local copies, waits for them, and re-layouts: 14.7 us -> none  [potential(): column_pass(flat_piece, weights, forward, backward)]
    dot_general x4 -> x2, matrix products: 17.3 us -> 2.95 us  [the longest x1 1.55 us: column_weights(): lax.dot_general(one_hot(column_y, own_y), one_hot(column_x, inner_freq),...]
    all_to_all x1, blocking collectives: 41.8 us -> 27.7 us  [local(): scaled = lax.all_to_all(scaled, 'fft', 0, 0, tiled=True)]
    slice x3 -> x0, local copies, waits for them, and re-layouts: 13.5 us -> none  [the longest x2 8.33 us: action_of(): imag_field = field[:, :, 1]]
  transfers between devices with their start and end apart: 2 -> 2, of which waited for: 1 -> 2; matrix products, arithmetic and copies ran while one was open for 58% -> 8% of each run, Pallas kernels for 0% -> 0%
where the time goes in v1:
time: 132 us; the launch traced here: 131 us
  waiting for transfers between devices  61.8 us (47%)
  blocking collectives  27.7 us (21%)
  Pallas kernels  18.5 us (14%)
  starting transfers between devices  6.77 us (5%)
  local copies, waits for them, and re-layouts  6.69 us (5%)
  other arithmetic  6.53 us (5%)
  matrix products  2.95 us (2%)
    ppermute x1, waiting for transfers between devices, shifted(): return lax.ppermute(value, axis, pairs)  44.2 us
    all_to_all x1, blocking collectives, local(): scaled = lax.all_to_all(scaled, 'fft', 0, 0, tiled=True)  27.7 us
    all_to_all x1, waiting for transfers between devices, local(): spectrum = lax.all_to_all(spectrum, 'fft', 0, 0, tiled=True)  17.7 us
    pallas_call x1, Pallas kernels, local(): pl.pallas_call(functools.partial(backward_kernel, planes=planes, fft_coun...  7.29 us
    pallas_call x1, Pallas kernels, local(): pl.pallas_call(functools.partial(forward_kernel, planes=planes, fft_count...  6.75 us
    unnamed x20, local copies, waits for them, and re-layouts  6.04 us
    pallas_call x1, Pallas kernels, local(): pl.pallas_call(functools.partial(column_kernel, fft_count=fft_count), out...  4.43 us
    all_to_all x1, starting transfers between devices, local(): spectrum = lax.all_to_all(spectrum, 'fft', 0, 0, tiled=True)  3.72 us
  transfers between devices with their start and end apart: 2, of which 2 were waited for; matrix products, arithmetic and copies ran while one was open for 8% of the time, Pallas kernels for 0%

profile of v1, /device:TPU:0, one launch (start us, length us, event | category | flops | bytes accessed | tf_op | source)
XLA Modules:
  0.0 131.1 jit_solution(7945697716418187990)
XLA Ops:
  0.0 3.1 %collective-permute-start = (bf16[1,2,1,20,25600]{4,1,3,2,0:T(2,128)(2,1)}, bf16[1,2,1,20,25600]{4,1,3,2,0:T(2,128)(2,1)S(1)}, u32[]{:S(2)}, u32[]{:S(2)}) collective-permute-start(bf16[1,2,1,20,25600]{4,1,3,2,0:T(2,128)(2,1)} %param.11), channel_id=1, source_target_pairs={{0,8},{8,16},{16,24},{24,0},{1,9},{9,17},{17,25},{25,1},{2,10},{10... | collective-permute-start | bytes 6144008 | tf_op jit(solution)/shard_map/ppermute | solution.py:32
  3.1 0.8 select_reduce_fusion
  3.8 0.6 fusion.39
  4.5 0.9 fusion.22
  5.4 0.3 fusion.46
  5.7 44.2 %collective-permute-done = bf16[1,2,1,20,25600]{4,1,3,2,0:T(2,128)(2,1)S(1)} collective-permute-done((bf16[1,2,1,20,25600]{4,1,3,2,0:T(2,128)(2,1)}, bf16[1,2,1,20,25600]{4,1,3,2,0:T(2,128)(2,1)S(1)}, u32[]{:S(2)}, u32[]{:S(2)}) %collective-permute-start) | collective-permute-done | bytes 2048032 | tf_op jit(solution)/shard_map/ppermute | solution.py:32
  49.9 1.3 copy-done
  51.2 1.6 %copy-done.3 = bf16[1,2,1,20,25600]{4,1,3,2,0:T(2,128)(2,1)S(1)} copy-done((bf16[1,2,1,20,25600]{4,1,3,2,0:T(2,128)(2,1)S(1)}, bf16[1,2,1,20,25600]{4,1,3,2,0:T(2,128)(2,1)}, u32[]{:S(2)}) %copy-start.3) | copy-done | bytes 2048024
  52.7 0.9 copy-done.4
  53.7 0.9 copy-done.9
  54.6 6.8 %density_xy.1 = bf16[8,20,48,128]{3,2,1,0:T(8,128)(2,1)S(1)} custom-call(bf16[8000,128]{1,0:T(8,128)(2,1)S(1)} %bitcast.23, bf16[8000,128]{1,0:T(8,128)(2,1)} %bitcast.21, bf16[4,512,512]{2,1,0:T(8,128)(2,1)} %constant.170.x_ref, bf16[320,320]{1,0:T(8,128)(2,1)S(1)} %copy-done.9, bf16[320,256]{1,0:T(8,128)(2,1)S(1)} %copy-done.4), custom_call_target="tpu_custom_call" | custom-call | tf_op jit(solution)/shard_map/density_xy/pallas_call | solution.py:335
  61.4 1.3 copy-done.2
  62.7 3.7 %all-to-all-start = ((bf16[8,20,48,128]{3,2,1,0:T(8,128)(2,1)}), bf16[8,20,48,128]{3,2,1,0:T(8,128)(2,1)S(1)}, u32[]{:S(2)}, u32[]{:S(2)}) async-start(bf16[8,20,48,128]{3,2,1,0:T(8,128)(2,1)} %copy-done.2), calls=%async_computation | async-start | bytes 3932160 | tf_op jit(solution)/shard_map/all_to_all | solution.py:345
  66.4 0.6 add_multiply_fusion.1
  67.0 1.4 %fusion.2 = f32[4,128]{1,0:T(4,128)S(1)} fusion(s32[16000]{0:T(1024)S(1)} %get-tuple-element.8, s32[128]{0:T(128)S(1)} %compare_select_fusion.4, s32[16000]{0:T(1024)S(1)} %get-tuple-element.7, s32[4]{0:T(128)S(1)} %iota_add_fusion), kind=kOutput, calls=%fused_computation.2 | convolution fusion | flops 18496000 | bytes 130576 | tf_op jit(solution)/shard_map/dot_general | solution.py:131
  68.4 1.5 %fusion = f32[20,128]{1,0:T(8,128)S(1)} fusion(s32[16000]{0:T(1024)S(1)} %get-tuple-element.7, s32[128]{0:T(128)S(1)} %compare_select_fusion.4, pred[20,16000]{1,0:T(8,128)(4,1)S(1)} %fusion.46), kind=kOutput, calls=%fused_computation | convolution fusion | flops 83968000 | bytes 394752 | tf_op jit(solution)/shard_map/dot_general | solution.py:128
  70.0 0.1 fusion.37
  70.1 1.2 multiply_add_fusion
  71.3 2.6 %fusion.13.weight_ref = f32[160,3072]{1,0:T(8,128)} fusion(f32[3072]{0:T(1024)S(1)} %multiply_add_fusion, f32[160]{0:T(256)S(1)} %add_multiply_fusion.1, s32[160]{0:T(256)S(1)} %fusion.38, s32[3072]{0:T(1024)S(1)} %multiply_add_fusion.1, pred[3072]{0:T(1024)(128)(4,1)S(1)} %fusion.37), kind=kLoop, calls=%fused_computation.15 | loop fusion | flops 5406720 | bytes 1995008 | tf_op jit(solution)/shard_map/jit(_where)/select_n | solution.py:103
  73.9 17.7 %all-to-all-done.in_ref = bf16[8,20,48,128]{3,2,1,0:T(8,128)(2,1)S(1)} async-done(((bf16[8,20,48,128]{3,2,1,0:T(8,128)(2,1)}), bf16[8,20,48,128]{3,2,1,0:T(8,128)(2,1)S(1)}, u32[]{:S(2)}, u32[]{:S(2)}) %all-to-all-start) | async-done | bytes 1966112 | tf_op jit(solution)/shard_map/all_to_all | solution.py:345
  91.6 4.4 %columns.1 = bf16[8,24,40,128]{3,2,1,0:T(8,128)(2,1)S(1)} custom-call(bf16[8,20,48,128]{3,2,1,0:T(8,128)(2,1)S(1)} %all-to-all-done.in_ref, f32[160,3072]{1,0:T(8,128)} %fusion.13.weight_ref, bf16[320,320]{1,0:T(8,128)(2,1)S(1)} %copy-done.7, bf16[320,320]{1,0:T(8,128)(2,1)S(1)} %copy-done.8), custom_call_target="tpu_custom_call" | custom-call | tf_op jit(solution)/shard_map/columns/pallas_call | solution.py:346
  96.0 0.0 copy-start.5
  96.1 27.7 %all_to_all.10.in_ref = bf16[8,24,40,128]{3,2,1,0:T(8,128)(2,1)S(1)} all-to-all(bf16[8,24,40,128]{3,2,1,0:T(8,128)(2,1)S(1)} %columns.1), channel_id=1, replica_groups=mesh['pool'=4,'fft'=8] {'fft'}, dimensions={0} | all-to-all | bytes 3932160 | tf_op jit(solution)/shard_map/all_to_all | solution.py:353
  123.8 7.3 %yx_action.1 = bf16[8000,128]{1,0:T(8,128)(2,1)} custom-call(bf16[8,24,40,128]{3,2,1,0:T(8,128)(2,1)S(1)} %all_to_all.10.in_ref, bf16[8000,128]{1,0:T(8,128)(2,1)S(1)} %bitcast.22, bf16[4,512,512]{2,1,0:T(8,128)(2,1)} %constant.179.x_ref, bf16[320,320]{1,0:T(8,128)(2,1)S(1)} %copy-done.6, bf16[320,256]{1,0:T(8,128)(2,1)S(1)} %copy-done.5), custom_call_target="tpu_custom_call" | custom-call | tf_op jit(solution)/shard_map/yx_action/pallas_call | solution.py:354
  (21 shorter events, 0.1 us)
Async XLA Ops:
  0.0 49.9 %collective-permute-start = (bf16[1,2,1,20,25600]{4,1,3,2,0:T(2,128)(2,1)}, bf16[1,2,1,20,25600]{4,1,3,2,0:T(2,128)(2,1)S(1)}, u32[]{:S(2)}, u32[]{:S(2)}) collective-permute-start(bf16[1,2,1,20,25600]{4,1,3,2,0:T(2,128)(2,1)} %param.11), channel_id=1, source_target_pairs={{0,8},{8,16},{16,24},{24,0},{1,9},{9,17},{17,25},{25,1},{2,10},{10... | collective-permute-start | bytes 6144008 | tf_op jit(solution)/shard_map/ppermute | solution.py:32
  49.9 1.3 copy-start
  51.2 1.6 %copy-start.3 = (bf16[1,2,1,20,25600]{4,1,3,2,0:T(2,128)(2,1)S(1)}, bf16[1,2,1,20,25600]{4,1,3,2,0:T(2,128)(2,1)}, u32[]{:S(2)}) copy-start(bf16[1,2,1,20,25600]{4,1,3,2,0:T(2,128)(2,1)} %param.11) | copy-start | bytes 6144004
  52.7 0.9 copy-start.4
  53.7 0.9 copy-start.9
  61.4 1.3 copy-start.2
  62.7 28.9 %all-to-all-start = ((bf16[8,20,48,128]{3,2,1,0:T(8,128)(2,1)}), bf16[8,20,48,128]{3,2,1,0:T(8,128)(2,1)S(1)}, u32[]{:S(2)}, u32[]{:S(2)}) async-start(bf16[8,20,48,128]{3,2,1,0:T(8,128)(2,1)} %copy-done.2), calls=%async_computation | async-start | bytes 3932160 | tf_op jit(solution)/shard_map/all_to_all | solution.py:345
  68.4 23.2 %copy-start.7 = (bf16[320,320]{1,0:T(8,128)(2,1)S(1)}, bf16[320,320]{1,0:T(8,128)(2,1)}, u32[]{:S(2)}) copy-start(bf16[320,320]{1,0:T(8,128)(2,1)} %constant.142.clone.fwd_ref) | copy-start | bytes 614404
  68.4 23.2 %copy-start.8 = (bf16[320,320]{1,0:T(8,128)(2,1)S(1)}, bf16[320,320]{1,0:T(8,128)(2,1)}, u32[]{:S(2)}) copy-start(bf16[320,320]{1,0:T(8,128)(2,1)} %constant.143.clone.bwd_ref) | copy-start | bytes 614404
  96.0 27.8 %copy-start.1 = (bf16[1,2,1,20,25600]{4,1,3,2,0:T(2,128)(2,1)S(1)}, bf16[1,2,1,20,25600]{4,1,3,2,0:T(2,128)(2,1)}, u32[]{:S(2)}) copy-start(bf16[1,2,1,20,25600]{4,1,3,2,0:T(2,128)(2,1)} %copy-done) | copy-start | bytes 6144004
  96.0 27.7 %copy-start.5 = (bf16[320,256]{1,0:T(8,128)(2,1)S(1)}, bf16[320,256]{1,0:T(8,128)(2,1)}, u32[]{:S(2)}) copy-start(bf16[320,256]{1,0:T(8,128)(2,1)} %constant.141.clone.side_ref) | copy-start | bytes 491524
  96.0 27.7 %copy-start.6 = (bf16[320,320]{1,0:T(8,128)(2,1)S(1)}, bf16[320,320]{1,0:T(8,128)(2,1)}, u32[]{:S(2)}) copy-start(bf16[320,320]{1,0:T(8,128)(2,1)} %constant.144.clone.y_ref) | copy-start | bytes 614404

commit v2 on v1

--- a/solution.py
+++ b/solution.py
@@ -8,6 +8,7 @@
 from jax.experimental import pallas as pl
 from jax.experimental.pallas import tpu as pltpu
 from jax.sharding import PartitionSpec as P
+
 
 NG = 160
 KMESH = 4
@@ -53,33 +54,43 @@
     return np.take(table, range(HALF, table.shape[axis] - HALF), axis)
 
 
-def padded(table, axis, size):
-    widths = [(0, 0)] * table.ndim
-    widths[axis] = (0, size - table.shape[axis])
-    return np.pad(table, widths)
-
-
-def tables(fft_count):
+def met(table, axis, rank):
+    count = table.shape[axis]
+    bits = count.bit_length() - 1
+    split = table.reshape(table.shape[:axis] + (2,) * bits + table.shape[axis + 1 :])
+    for bit in range(bits):
+        swapped = jnp.flip(split, axis + bits - 1 - bit)
+        split = jnp.where((rank >> bit) & 1 == 1, swapped, split)
+    return split.reshape(table.shape)
+
+
+def tables(fft_count, rank, chunks):
     share = NG // fft_count
+    side_share = OUTER // fft_count
     fwd = dft_table(NG, -1.0)
     bwd = dft_table(NG, 1.0)
     full = 2 * NG
-    x_fwd = np.concatenate(
-        [inner(fwd, 3).reshape(2, NG, 2 * LANES), padded(outer(fwd, 3), 3, LANES).reshape(2, NG, 2 * LANES)], 2
-    )
-    x_bwd = np.concatenate(
-        [inner(bwd, 1).reshape(2 * LANES, 2, NG), padded(outer(bwd, 1), 1, LANES).reshape(2 * LANES, 2, NG)], 0
-    )
+    cast = lambda t: jnp.asarray(t.astype(np.float32).astype(jnp.bfloat16))
+    side = met(cast(outer(fwd, 3).reshape(2, NG, 2, fft_count, side_share)), 3, rank).reshape(2, NG, 2, OUTER)
+    side = jnp.pad(side, ((0, 0), (0, 0), (0, 0), (0, LANES - OUTER))).reshape(2, NG, 2 * LANES)
+    x_fwd = jnp.concatenate([cast(inner(fwd, 3)).reshape(2, NG, 2 * LANES), side], 2)
+    side = met(cast(outer(bwd, 1).reshape(2, fft_count, side_share, 2, NG)), 1, rank).reshape(2, OUTER, 2, NG)
+    side = jnp.pad(side, ((0, 0), (0, LANES - OUTER), (0, 0), (0, 0))).reshape(2 * LANES, 2, NG)
+    x_bwd = jnp.concatenate([cast(inner(bwd, 1)).reshape(2 * LANES, 2, NG), side], 0)
     split = fwd.reshape(2, GROUPS, GROUP, 2, fft_count, share)
-    y_fwd = split.transpose(4, 3, 5, 0, 2, 1).reshape(full, full)
-    y_fwd_side = inner(fwd.reshape(2, GROUPS, GROUP, 2, NG).transpose(0, 2, 1, 3, 4), 4).reshape(full, 2 * LANES)
-    z_fwd = fwd.transpose(2, 3, 0, 1).reshape(full, full)
-    z_bwd = bwd.reshape(2, NG, 2, fft_count, share).transpose(3, 2, 4, 0, 1).reshape(full, full)
+    y_fwd = met(cast(split.transpose(4, 3, 5, 0, 2, 1)), 0, rank).reshape(full, full)
+    y_fwd_side = cast(inner(fwd.reshape(2, GROUPS, GROUP, 2, NG).transpose(0, 2, 1, 3, 4), 4)).reshape(full, 2 * LANES)
+    edges = np.cumsum([0] + chunks)
+    spans = list(zip(edges[:-1], edges[1:]))
+    z_fwd = fwd.reshape(2, fft_count, share, full).transpose(3, 0, 1, 2)
+    z_fwd = met(cast(z_fwd), 2, rank)
+    z_fwd = jnp.concatenate([z_fwd[:, :, :, a:b].reshape(full, 2, -1) for a, b in spans], 2).reshape(full, full)
+    z_bwd = met(cast(bwd.reshape(2, NG, 2, fft_count, share).transpose(3, 2, 4, 0, 1)), 0, rank)
+    z_bwd = jnp.concatenate([z_bwd[:, :, a:b].reshape(-1, full) for a, b in spans], 0)
     order = bwd.reshape(2, NG, 2, GROUPS, GROUP).transpose(2, 4, 3, 0, 1)
-    y_bwd = order.reshape(full, full)
-    y_bwd_side = inner(order, 4).reshape(full, 2 * LANES)
-    cast = lambda t: jnp.asarray(t.astype(np.float32).astype(jnp.bfloat16))
-    return [cast(t) for t in (x_fwd, x_bwd, y_fwd, y_fwd_side, z_fwd, z_bwd, y_bwd, y_bwd_side)]
+    y_bwd = met(cast(order.reshape(full, 2, fft_count, share)), 2, rank).reshape(full, full)
+    y_bwd_side = cast(inner(order, 4)).reshape(full, 2 * LANES)
+    return x_fwd, x_bwd, y_fwd, y_fwd_side, z_fwd, z_bwd, y_bwd, y_bwd_side
 
 
 def signed(frequency, grid_size):
@@ -153,7 +164,10 @@
     return [tuple(range(i, min(i + 2, count))) for i in range(0, count, 2)]
 
 
-def forward_kernel(own_ref, recv_ref, x_ref, y_ref, side_ref, out_ref, own_f, recv_f, *, planes, fft_count):
+def forward_kernel(*refs, planes, fft_count):
+    own_ref, recv_ref, x_ref, y_ref, side_ref = refs[:5]
+    out_refs = refs[5:-2]
+    own_f, recv_f = refs[-2:]
     share = NG // fft_count
     side_share = OUTER // fft_count
     own_f[...] = own_ref[...].astype(jnp.float32)
@@ -185,7 +199,7 @@
         along_y = dot(y_ref[...], right)
         for n, z in enumerate(pair):
             for k in range(fft_count):
-                out_ref[k, z, : 2 * share, :] = along_y[
+                out_refs[k][z, : 2 * share, :] = along_y[
                     2 * share * k : 2 * share * (k + 1), n * LANES : (n + 1) * LANES
                 ].astype(jnp.bfloat16)
     side = stacked(0, 2)
@@ -196,16 +210,25 @@
     for z in range(planes):
         for k in range(fft_count):
             row = z * OUTER + k * side_share
-            out_ref[k, z, 2 * share :, :] = jnp.concatenate(
+            out_refs[k][z, 2 * share :, :] = jnp.concatenate(
                 [side_y[row : row + side_share, c * LANES : (c + 1) * LANES] for c in range(2)], axis=0
             ).astype(jnp.bfloat16)
 
 
-def column_kernel(in_ref, weight_ref, fwd_ref, bwd_ref, out_ref, wide, *, fft_count):
+def column_kernel(*refs, fft_count, chunks):
+    count = fft_count * len(chunks)
+    in_refs = refs[:count]
+    weight_ref, fwd_ref, bwd_ref = refs[count : count + 3]
+    out_refs = refs[count + 3 : -1]
+    wide = refs[-1]
     share = NG // fft_count
     side_share = OUTER // fft_count
     height = 2 * (share + side_share)
-    wide[...] = in_ref[...].reshape(NG * height, LANES).astype(jnp.float32)
+    first = 0
+    for in_ref in in_refs:
+        rows = in_ref.shape[0] * height
+        wide[first : first + rows, :] = in_ref[...].reshape(rows, LANES).astype(jnp.float32)
+        first += rows
 
     def column(i):
         first = i if i < share else 2 * share + i - share
@@ -219,40 +242,42 @@
         scaled = jnp.concatenate([spectrum[:NG] * weight, spectrum[NG:] * weight], axis=0).astype(jnp.bfloat16)
         back = dot(bwd_ref[...], scaled)
         for n, i in enumerate(pair):
-            for k in range(fft_count):
-                out_ref[k, i, :, :] = back[
-                    2 * share * k : 2 * share * (k + 1), n * LANES : (n + 1) * LANES
-                ].astype(jnp.bfloat16)
-
-
-def backward_kernel(
-    in_ref, recv_ref, x_ref, y_ref, side_ref, out_ref, main_f, side_f, recv_f, out_f, *, planes, fft_count
-):
+            first = 0
+            for out_ref in out_refs:
+                rows = out_ref.shape[1]
+                out_ref[i, :, :] = back[first : first + rows, n * LANES : (n + 1) * LANES].astype(jnp.bfloat16)
+                first += rows
+
+
+def backward_kernel(*refs, planes, depth, fft_count):
+    in_refs = refs[:fft_count]
+    recv_ref, x_ref, y_ref, side_ref = refs[fft_count : fft_count + 4]
+    out_ref, main_f, side_f, recv_f, out_f = refs[-5:]
     share = NG // fft_count
     side_share = OUTER // fft_count
-    height = 2 * share
+    height = 2 * depth
 
     @pl.when(pl.program_id(0) == 0)
     def _():
         for k in range(fft_count):
-            main_f[pl.ds(k * share * height, share * height), :] = (
-                in_ref[k, :share].reshape(share * height, LANES).astype(jnp.float32)
+            main_f[k * share * height : (k + 1) * share * height, :] = (
+                in_refs[k][:share].reshape(share * height, LANES).astype(jnp.float32)
             )
-            side_f[pl.ds(k * side_share * height, side_share * height), :] = (
-                in_ref[k, share:].reshape(side_share * height, LANES).astype(jnp.float32)
+            side_f[k * side_share * height : (k + 1) * side_share * height, :] = (
+                in_refs[k][share:].reshape(side_share * height, LANES).astype(jnp.float32)
             )
 
+    base = pl.program_id(0) * planes
     recv_f[...] = recv_ref[...].astype(jnp.float32)
-    base = pl.program_id(0) * planes
 
     def main_of(z):
         return jnp.concatenate(
-            [main_f[pl.ds(base + z + c * share, NG, stride=height), :] for c in range(2)], axis=0
+            [main_f[pl.ds(base + z + c * depth, NG, stride=height), :] for c in range(2)], axis=0
         )
 
     def side_of(z):
         return jnp.concatenate(
-            [side_f[pl.ds(base + z + c * share, OUTER, stride=height), :] for c in range(2)], axis=1
+            [side_f[pl.ds(base + z + c * depth, OUTER, stride=height), :] for c in range(2)], axis=1
         )
 
     back_y = []
@@ -312,55 +337,86 @@
     return jnp.stack(placed)
 
 
+def exchange(parts):
+    count = len(parts)
+    moved = [parts[0]]
+    for m in range(1, count):
+        moved.append(lax.ppermute(parts[m], "fft", [(i, i ^ m) for i in range(count)]))
+    return moved
+
+
 def local(orbitals, stick_map, kpoint_grid):
-    moved = shifted(orbitals, "pool", 1)
     planes_all = orbitals.shape[3]
     planes = GROUP if planes_all % GROUP == 0 else 1
     steps = planes_all // planes
+    chunk_steps = [steps - steps // 2, steps // 2]
+    chunks = [count * planes for count in chunk_steps]
+    starts = [0, chunks[0]]
+    moved = []
+    for a, n in zip(starts, chunks):
+        moved.append(shifted(orbitals[:, :, :, a : a + n], "pool", 1))
     fft_count = lax.axis_size("fft")
     fft_rank = lax.axis_index("fft")
     share = NG // fft_count
     side_share = OUTER // fft_count
     columns = share + side_share
-    x_fwd, x_bwd, y_fwd, y_fwd_side, z_fwd, z_bwd, y_bwd, y_bwd_side = tables(fft_count)
+    x_fwd, x_bwd, y_fwd, y_fwd_side, z_fwd, z_bwd, y_bwd, y_bwd_side = tables(fft_count, fft_rank, chunks)
     x_fwd = x_windows(x_fwd, 1)
     x_bwd = x_windows(x_bwd, 2)
     weights = column_weights(stick_map, kpoint_grid, fft_rank, share, side_share)
     own = rows_of(orbitals)
-    received = rows_of(moved)
+    received = [rows_of(piece) for piece in moved]
     block = planes * ROWS
-    row_spec = pl.BlockSpec((block, LANES), lambda s: (s, 0))
+    row_spec = lambda first: pl.BlockSpec((block, LANES), lambda s: (first + s, 0))
     params = pltpu.CompilerParams(vmem_limit_bytes=48 << 20)
     wide = lambda count: pltpu.VMEM((count, LANES), jnp.float32)
-    spectrum = pl.pallas_call(
-        functools.partial(forward_kernel, planes=planes, fft_count=fft_count),
-        grid=(steps,),
-        in_specs=[row_spec, row_spec, whole(x_fwd.shape), whole(y_fwd.shape), whole(y_fwd_side.shape)],
-        out_specs=pl.BlockSpec((fft_count, planes, 2 * columns, LANES), lambda s: (0, s, 0, 0)),
-        out_shape=jax.ShapeDtypeStruct((fft_count, planes_all, 2 * columns, LANES), jnp.bfloat16),
-        scratch_shapes=[wide(block), wide(block)],
-        compiler_params=params,
-        name="density_xy",
-    )(own, received, x_fwd, y_fwd, y_fwd_side)
-    spectrum = lax.all_to_all(spectrum, "fft", 0, 0, tiled=True)
+    bf16 = lambda *shape: jax.ShapeDtypeStruct(shape, jnp.bfloat16)
+    spectra = []
+    for c, count in enumerate(chunk_steps):
+        spectrum = pl.pallas_call(
+            functools.partial(forward_kernel, planes=planes, fft_count=fft_count),
+            grid=(count,),
+            in_specs=[
+                row_spec(starts[c] // planes),
+                row_spec(0),
+                whole(x_fwd.shape),
+                whole(y_fwd.shape),
+                whole(y_fwd_side.shape),
+            ],
+            out_specs=[pl.BlockSpec((planes, 2 * columns, LANES), lambda s: (s, 0, 0))] * fft_count,
+            out_shape=[bf16(chunks[c], 2 * columns, LANES)] * fft_count,
+            scratch_shapes=[wide(block), wide(block)],
+            compiler_params=params,
+            name="density_xy",
+        )(own, received[c], x_fwd, y_fwd, y_fwd_side)
+        spectra += exchange(spectrum)
     scaled = pl.pallas_call(
-        functools.partial(column_kernel, fft_count=fft_count),
-        out_shape=jax.ShapeDtypeStruct((fft_count, columns, 2 * share, LANES), jnp.bfloat16),
+        functools.partial(column_kernel, fft_count=fft_count, chunks=chunks),
+        out_shape=[bf16(columns, 2 * depth, LANES) for depth in chunks for _ in range(fft_count)],
         scratch_shapes=[wide(NG * 2 * columns)],
         compiler_params=params,
         name="columns",
-    )(spectrum, weights, z_fwd, z_bwd)
-    scaled = lax.all_to_all(scaled, "fft", 0, 0, tiled=True)
-    result = pl.pallas_call(
-        functools.partial(backward_kernel, planes=planes, fft_count=fft_count),
-        grid=(steps,),
-        in_specs=[whole(scaled.shape), row_spec, whole(x_bwd.shape), whole(y_bwd.shape), whole(y_bwd_side.shape)],
-        out_specs=row_spec,
-        out_shape=jax.ShapeDtypeStruct((planes_all * ROWS, LANES), jnp.bfloat16),
-        scratch_shapes=[wide(NG * 2 * share), wide(OUTER * 2 * share), wide(block), wide(block)],
-        compiler_params=params,
-        name="yx_action",
-    )(scaled, received, x_bwd, y_bwd, y_bwd_side)
+    )(*spectra, weights, z_fwd, z_bwd)
+    returned = [exchange(scaled[c * fft_count : (c + 1) * fft_count]) for c in range(len(chunks))]
+    result = None
+    for c, count in enumerate(chunk_steps):
+        inputs = [*returned[c], received[c], x_bwd, y_bwd, y_bwd_side]
+        specs = [whole(piece.shape) for piece in returned[c]]
+        specs += [row_spec(0), whole(x_bwd.shape), whole(y_bwd.shape), whole(y_bwd_side.shape)]
+        if c > 0:
+            inputs.append(result)
+            specs.append(pl.BlockSpec(memory_space=pl.ANY))
+        result = pl.pallas_call(
+            functools.partial(backward_kernel, planes=planes, depth=chunks[c], fft_count=fft_count),
+            grid=(count,),
+            in_specs=specs,
+            out_specs=row_spec(starts[c] // planes),
+            out_shape=bf16(planes_all * ROWS, LANES),
+            scratch_shapes=[wide(NG * 2 * chunks[c]), wide(OUTER * 2 * chunks[c]), wide(block), wide(block)],
+            input_output_aliases={len(inputs) - 1: 0} if c > 0 else {},
+            compiler_params=params,
+            name="yx_action",
+        )(*inputs)
     result = result.reshape(planes_all, NG * NG // LANES, 2, LANES).transpose(2, 0, 1, 3)
     return result.reshape(orbitals.shape)
 

time: 132 us -> 145 us (1.098)
  local copies, waits for them, and re-layouts: 6.69 us -> 45.5 us
  waiting for transfers between devices: 61.8 us -> 28.4 us
  blocking collectives: 27.7 us -> 0 us
  starting transfers between devices: 6.77 us -> 31.2 us
  other arithmetic: 6.53 us -> 14.4 us
  Pallas kernels: 18.5 us -> 21.2 us
    all_to_all x1 -> x0, blocking collectives: 27.7 us -> none  [local(): scaled = lax.all_to_all(scaled, 'fft', 0, 0, tiled=True)]
    ppermute x0 -> x28, starting transfers between devices: none -> 26.6 us  [exchange(): lax.ppermute(parts[m], 'fft', [(i, i ^ m) for i in range(count)])]
    ppermute x1 -> x2, waiting for transfers between devices: 44.2 us -> 18.8 us  [shifted(): return lax.ppermute(value, axis, pairs)]
    all_to_all x1 -> x0, waiting for transfers between devices: 17.7 us -> none  [local(): spectrum = lax.all_to_all(spectrum, 'fft', 0, 0, tiled=True)]
    another operation x0 -> x8, local copies, waits for them, and re-layouts: none -> 11.7 us  [the longest x5 7.76 us: x_windows(): return jnp.stack(placed)]
    unnamed x20 -> x102, local copies, waits for them, and re-layouts: 6.04 us -> 16.2 us
    ppermute x0 -> x28, waiting for transfers between devices: none -> 9.67 us  [exchange(): lax.ppermute(parts[m], 'fft', [(i, i ^ m) for i in range(count)])]
    slice x0 -> x6, local copies, waits for them, and re-layouts: none -> 6.87 us  [the longest x2 5.82 us: local(): moved.append(shifted(orbitals[:, :, :, a:a + n], 'pool', 1))]
  transfers between devices with their start and end apart: 2 -> 30, of which waited for: 2 -> 6; matrix products, arithmetic and copies ran while one was open for 8% -> 33% of each run, Pallas kernels for 0% -> 9%
where the time goes in v2:
time: 145 us; the launch traced here: 144 us
  local copies, waits for them, and re-layouts  45.5 us (31%)
  starting transfers between devices  31.2 us (22%)
  waiting for transfers between devices  28.4 us (20%)
  Pallas kernels  21.2 us (15%)
  other arithmetic  14.4 us (10%)
  matrix products  2.92 us (2%)
    ppermute x28, starting transfers between devices, exchange(): lax.ppermute(parts[m], 'fft', [(i, i ^ m) for i in range(count)])  26.6 us
    ppermute x2, waiting for transfers between devices, shifted(): return lax.ppermute(value, axis, pairs)  18.8 us
    unnamed x102, local copies, waits for them, and re-layouts  16.2 us
    ppermute x28, waiting for transfers between devices, exchange(): lax.ppermute(parts[m], 'fft', [(i, i ^ m) for i in range(count)])  9.67 us
    pallas_call x2, Pallas kernels, local(): pl.pallas_call(functools.partial(forward_kernel, planes=planes, fft_count...  8.05 us
    pallas_call x2, Pallas kernels, local(): pl.pallas_call(functools.partial(backward_kernel, planes=planes, depth=ch...  8.02 us
    another operation x5, local copies, waits for them, and re-layouts, x_windows(): return jnp.stack(placed)  7.76 us
    slice x2, local copies, waits for them, and re-layouts, local(): moved.append(shifted(orbitals[:, :, :, a:a + n], 'pool', 1))  5.82 us
  transfers between devices with their start and end apart: 30, of which 6 were waited for; matrix products, arithmetic and copies ran while one was open for 33% of the time, Pallas kernels for 9%

profile of v2, /device:TPU:0, one launch (start us, length us, event | category | flops | bytes accessed | tf_op | source)
XLA Modules:
  0.0 144.4 jit_solution(15262599856688190648)
XLA Ops:
  0.0 2.7 %slice.28 = bf16[1,2,1,8,25600]{4,1,3,2,0:T(2,128)(2,1)} slice(bf16[1,2,1,20,25600]{4,1,3,2,0:T(2,128)(2,1)} %param.13), slice={[0:1], [0:2], [0:1], [12:20], [0:25600]} | slice | bytes 1638400 | tf_op jit(solution)/shard_map/slice | solution.py:357
  2.7 3.1 %collective-permute-start.8 = (bf16[1,2,1,8,25600]{4,1,3,2,0:T(2,128)(2,1)}, bf16[1,2,1,8,25600]{4,1,3,2,0:T(2,128)(2,1)S(1)}, u32[]{:S(2)}, u32[]{:S(2)}) collective-permute-start(bf16[1,2,1,8,25600]{4,1,3,2,0:T(2,128)(2,1)} %slice.28), channel_id=1, source_target_pairs={{0,8},{8,16},{16,24},{24,0},{1,9},{9,17},{17,25},{25,1},{2,10},{10... | collective-permute-start | bytes 2457608 | tf_op jit(solution)/shard_map/ppermute | solution.py:33
  5.7 3.2 %slice.27 = bf16[1,2,1,12,25600]{4,1,3,2,0:T(2,128)(2,1)} slice(bf16[1,2,1,20,25600]{4,1,3,2,0:T(2,128)(2,1)} %param.13), slice={[0:1], [0:2], [0:1], [0:12], [0:25600]} | slice | bytes 2457600 | tf_op jit(solution)/shard_map/slice | solution.py:357
  24.5 2.7 %fusion.13.refs_16_ = f32[160,3072]{1,0:T(8,128)} fusion(f32[3072]{0:T(1024)S(1)} %multiply_add_fusion, f32[160]{0:T(256)S(1)} %add_multiply_fusion.1, s32[160]{0:T(256)S(1)} %fusion.38, s32[3072]{0:T(1024)S(1)} %multiply_add_fusion.1, pred[3072]{0:T(1024)(128)(4,1)S(1)} %fusion.37), kind=kLoop, calls=%fused_computation.16 | loop fusion | flops 5406720 | bytes 1995008 | tf_op jit(solution)/shard_map/jit(_where)/select_n | solution.py:114
  27.2 2.8 %density_xy.3 = (bf16[8,48,128]{2,1,0:T(8,128)(2,1)S(1)}, bf16[8,48,128]{2,1,0:T(8,128)(2,1)S(1)}, bf16[8,48,128]{2,1,0:T(8,128)(2,1)S(1)}, bf16[8,48,128]{2,1,0...) custom-call(bf16[8000,128]{1,0:T(8,128)(2,1)S(1)} %bitcast.53, ...), custom_call_target="tpu_custom_call" | custom-call | tf_op jit(solution)/shard_map/density_xy/pallas_call | solution.py:376
  30.1 1.6 %collective-permute-start.10 = (bf16[8,48,128]{2,1,0:T(8,128)(2,1)S(1)}, bf16[8,48,128]{2,1,0:T(8,128)(2,1)S(1)}, u32[]{:S(2)}, u32[]{:S(2)}) collective-permute-start(bf16[8,48,128]{2,1,0:T(8,128)(2,1)S(1)} %get-tuple-element.47), channel_id=1, source_target_pairs={{0,2},{1,3},{2,0},{3,1},{4,6},{5,7},{6,4},{7,5},{8,10},{9,11},{10,... | collective-permute-start | bytes 294920 | tf_op jit(solution)/shard_map/ppermute | solution.py:344
  33.7 18.8 %collective-permute-done = bf16[1,2,1,12,25600]{4,1,3,2,0:T(2,128)(2,1)S(1)} collective-permute-done((bf16[1,2,1,12,25600]{4,1,3,2,0:T(2,128)(2,1)}, bf16[1,2,1,12,25600]{4,1,3,2,0:T(2,128)(2,1)S(1)}, u32[]{:S(2)}, u32[]{:S(2)}) %collective-permute-start) | collective-permute-done | bytes 1228832 | tf_op jit(solution)/shard_map/ppermute | solution.py:33
  52.5 5.2 %density_xy.2 = (bf16[12,48,128]{2,1,0:T(8,128)(2,1)S(1)}, bf16[12,48,128]{2,1,0:T(8,128)(2,1)S(1)}, bf16[12,48,128]{2,1,0:T(8,128)(2,1)S(1)}, bf16[12,48,128]{2...) custom-call(bf16[8000,128]{1,0:T(8,128)(2,1)S(1)} %bitcast.54, ...), custom_call_target="tpu_custom_call" | custom-call | tf_op jit(solution)/shard_map/density_xy/pallas_call | solution.py:376
  62.6 1.7 %reshape.195 = bf16[128,320]{1,0:T(8,128)(2,1)} reshape(bf16[8,2,8,2,160]{4,3,2,1,0:T(2,128)(2,1)} %slice.39) | data formatting | bytes 163840 | tf_op jit(solution)/shard_map/reshape | solution.py:89
  68.6 1.8 %collective-permute-done.14.refs_14_ = bf16[8,48,128]{2,1,0:T(8,128)(2,1)S(1)} collective-permute-done((bf16[8,48,128]{2,1,0:T(8,128)(2,1)S(1)}, bf16[8,48,128]{2,1,0:T(8,128)(2,1)S(1)}, u32[]{:S(2)}, u32[]{:S(2)}) %collective-permute-start.14) | collective-permute-done | bytes 98336 | tf_op jit(solution)/shard_map/ppermute | solution.py:344
  74.0 2.6 %collective-permute-start.6 = (bf16[12,48,128]{2,1,0:T(8,128)(2,1)}, bf16[12,48,128]{2,1,0:T(8,128)(2,1)S(1)}, u32[]{:S(2)}, u32[]{:S(2)}) collective-permute-start(bf16[12,48,128]{2,1,0:T(8,128)(2,1)} %get-tuple-element.43), channel_id=1, source_target_pairs={{0,6},{1,7},{2,4},{3,5},{4,2},{5,3},{6,0},{7,1},{8,14},{9,15},{10,... | collective-permute-start | bytes 442376 | tf_op jit(solution)/shard_map/ppermute | solution.py:344
  79.9 1.7 %pad_maximum_fusion.1 = bf16[512,2,160]{2,1,0:T(2,128)(2,1)S(1)} fusion(bf16[256,2,160]{2,1,0:T(2,128)(2,1)S(1)} %bitcast.69, bf16[256,2,160]{2,1,0:T(2,128)(2,1)} %constant.184), kind=kLoop, calls=%fused_computation.28 | loop fusion | flops 163840 | bytes 655360 | tf_op jit(solution)/shard_map/concatenate | solution.py:79
  81.6 4.1 %collective-permute-done.4.refs_4_ = bf16[12,48,128]{2,1,0:T(8,128)(2,1)S(1)} collective-permute-done((bf16[12,48,128]{2,1,0:T(8,128)(2,1)}, bf16[12,48,128]{2,1,0:T(8,128)(2,1)S(1)}, u32[]{:S(2)}, u32[]{:S(2)}) %collective-permute-start.4) | collective-permute-done | bytes 147488 | tf_op jit(solution)/shard_map/ppermute | solution.py:344
  85.7 1.6 %collective-permute-done.5.refs_5_ = bf16[12,48,128]{2,1,0:T(8,128)(2,1)S(1)} collective-permute-done((bf16[12,48,128]{2,1,0:T(8,128)(2,1)}, bf16[12,48,128]{2,1,0:T(8,128)(2,1)S(1)}, u32[]{:S(2)}, u32[]{:S(2)}) %collective-permute-start.5) | collective-permute-done | bytes 147488 | tf_op jit(solution)/shard_map/ppermute | solution.py:344
  90.9 5.2 %columns.1 = (bf16[24,24,128]{2,1,0:T(8,128)(2,1)S(1)}, bf16[24,24,128]{2,1,0:T(8,128)(2,1)}, bf16[24,24,128]{2,1,0:T(8,128)(2,1)}, bf16[24,24,128]{2,1,0:T(8,12...) custom-call(bf16[12,48,128]{2,1,0:T(8,128)(2,1)S(1)} %get-tuple-elem, ...), custom_call_target="tpu_custom_call" | custom-call | tf_op jit(solution)/shard_map/columns/pallas_call | solution.py:393
  105.2 3.1 %fusion.39 = (bf16[512,2,256]{2,1,0:T(2,128)(2,1)}, bf16[512,2,256]{2,1,0:T(2,128)(2,1)}, bf16[512,2,256]{2,1,0:T(2,128)(2,1)S(1)}, bf16[512,2,256]{2,1,0:T(2,128)(2,1)S(1)}) fusion(bf16[512,2,160]{2,1,0:T(2,128)(2,1)S(1)} %pad_maximum_fusion.1), kind=kLoop, calls=%fused_computation.95 | loop fusion | bytes 2424832 | tf_op jit(solution)/shard_map/jit(_pad)/pad | solution.py:336
  117.6 2.8 %collective-permute-start.29 = (bf16[24,24,128]{2,1,0:T(8,128)(2,1)}, bf16[24,24,128]{2,1,0:T(8,128)(2,1)}, u32[]{:S(2)}, u32[]{:S(2)}) collective-permute-start(bf16[24,24,128]{2,1,0:T(8,128)(2,1)} %copy-done.22), channel_id=1, source_target_pairs={{0,7},{1,6},{2,5},{3,4},{4,3},{5,2},{6,1},{7,0},{8,15},{9,14},{10,... | collective-permute-start | bytes 442376 | tf_op jit(solution)/shard_map/ppermute | solution.py:344
  121.5 2.2 %stack_reshape.30 = bf16[1,512,512]{2,1,0:T(8,128)(2,1)} reshape(bf16[512,2,256]{2,1,0:T(2,128)(2,1)} %get-tuple-element.72) | data formatting | bytes 1048576 | tf_op jit(solution)/shard_map/stack;reshape | solution.py:337
  123.7 2.2 %stack_reshape.31 = bf16[1,512,512]{2,1,0:T(8,128)(2,1)} reshape(bf16[512,2,256]{2,1,0:T(2,128)(2,1)} %get-tuple-element.71) | data formatting | bytes 1048576 | tf_op jit(solution)/shard_map/stack;reshape | solution.py:337
  125.9 1.7 %reshape_reshape.15 = bf16[320,320]{0,1:T(8,128)(2,1)} reshape(bf16[320,2,2,2,2,20]{0,5,4,3,2,1:T(8,128)(2,1)} %reverse_select_fusion.2) | data formatting | bytes 409600 | tf_op jit(solution)/shard_map/reshape;reshape | solution.py:91
  127.7 1.8 %copy.38.refs_10_ = bf16[320,320]{1,0:T(8,128)(2,1)} copy(bf16[320,320]{0,1:T(8,128)(2,1)} %reshape_reshape.15) | data formatting | bytes 409600 | tf_op jit(solution)/shard_map/reshape;reshape | solution.py:91
  132.2 1.8 %collective-permute-start.21 = (bf16[24,16,128]{2,1,0:T(8,128)(2,1)}, bf16[24,16,128]{2,1,0:T(8,128)(2,1)S(1)}, u32[]{:S(2)}, u32[]{:S(2)}) collective-permute-start(bf16[24,16,128]{2,1,0:T(8,128)(2,1)} %copy-done.29), channel_id=1, source_target_pairs={{0,6},{1,7},{2,4},{3,5},{4,2},{5,3},{6,0},{7,1},{8,14},{9,15},{10,... | collective-permute-start | bytes 294920 | tf_op jit(solution)/shard_map/ppermute | solution.py:344
  136.3 5.1 %yx_action.2.refs_12_ = bf16[8000,128]{1,0:T(8,128)(2,1)} custom-call(bf16[24,24,128]{2,1,0:T(8,128)(2,1)S(1)} %copy-done.7, bf16[24,24,128]{2,1,0:T(8,128)(2,1)} %collective-permute-done.23.refs_1_, bf16[24,24,128]{2,1,0:T(8,128)(2,1)} %collective-permute-done.24.refs_2_, bf16[24,24,128]{2,1,0:T(8,128)(2,1)} %collective-permute-done.25.refs_3_, ...), custom_call_target="tpu_custom_call" | custom-call | tf_op jit(solution)/shard_map/yx_action/pallas_call | solution.py:409
  141.5 2.9 %yx_action.3 = bf16[8000,128]{1,0:T(8,128)(2,1)} custom-call(bf16[24,16,128]{2,1,0:T(8,128)(2,1)S(1)} %copy-done.9, bf16[24,16,128]{2,1,0:T(8,128)(2,1)S(1)} %copy-done.11, bf16[24,16,128]{2,1,0:T(8,128)(2,1)S(1)} %copy-done.13, bf16[24,16,128]{2,1,0:T(8,128)(2,1)S(1)} %collective-permute-done.18.refs_3_, ...), custom_call_target="tpu_custom_call", output_to_operand_aliasing={{}: (12, {})} | custom-call | tf_op jit(solution)/shard_map/yx_action/pallas_call | solution.py:409
  (207 shorter events, 61.3 us)
Async XLA Ops:
  2.7 24.5 %collective-permute-start.8 = (bf16[1,2,1,8,25600]{4,1,3,2,0:T(2,128)(2,1)}, bf16[1,2,1,8,25600]{4,1,3,2,0:T(2,128)(2,1)S(1)}, u32[]{:S(2)}, u32[]{:S(2)}) collective-permute-start(bf16[1,2,1,8,25600]{4,1,3,2,0:T(2,128)(2,1)} %slice.28), channel_id=1, source_target_pairs={{0,8},{8,16},{16,24},{24,0},{1,9},{9,17},{17,25},{25,1},{2,10},{10... | collective-permute-start | bytes 2457608 | tf_op jit(solution)/shard_map/ppermute | solution.py:33
  8.9 43.6 %collective-permute-start = (bf16[1,2,1,12,25600]{4,1,3,2,0:T(2,128)(2,1)}, bf16[1,2,1,12,25600]{4,1,3,2,0:T(2,128)(2,1)S(1)}, u32[]{:S(2)}, u32[]{:S(2)}) collective-permute-start(bf16[1,2,1,12,25600]{4,1,3,2,0:T(2,128)(2,1)} %slice.27), channel_id=1, source_target_pairs={{0,8},{8,16},{16,24},{24,0},{1,9},{9,17},{17,25},{25,1},{2,10},{10... | collective-permute-start | bytes 3686408 | tf_op jit(solution)/shard_map/ppermute | solution.py:33
  30.1 28.3 %collective-permute-start.10 = (bf16[8,48,128]{2,1,0:T(8,128)(2,1)S(1)}, bf16[8,48,128]{2,1,0:T(8,128)(2,1)S(1)}, u32[]{:S(2)}, u32[]{:S(2)}) collective-permute-start(bf16[8,48,128]{2,1,0:T(8,128)(2,1)S(1)} %get-tuple-element.47), channel_id=1, source_target_pairs={{0,2},{1,3},{2,0},{3,1},{4,6},{5,7},{6,4},{7,5},{8,10},{9,11},{10,... | collective-permute-start | bytes 294920 | tf_op jit(solution)/shard_map/ppermute | solution.py:344
  31.7 32.6 %collective-permute-start.11 = (bf16[8,48,128]{2,1,0:T(8,128)(2,1)}, bf16[8,48,128]{2,1,0:T(8,128)(2,1)S(1)}, u32[]{:S(2)}, u32[]{:S(2)}) collective-permute-start(bf16[8,48,128]{2,1,0:T(8,128)(2,1)} %get-tuple-element.48), channel_id=1, source_target_pairs={{0,3},{1,2},{2,1},{3,0},{4,7},{5,6},{6,5},{7,4},{8,11},{9,10},{10,... | collective-permute-start | bytes 294920 | tf_op jit(solution)/shard_map/ppermute | solution.py:344
  31.8 34.0 %collective-permute-start.12 = (bf16[8,48,128]{2,1,0:T(8,128)(2,1)}, bf16[8,48,128]{2,1,0:T(8,128)(2,1)S(1)}, u32[]{:S(2)}, u32[]{:S(2)}) collective-permute-start(bf16[8,48,128]{2,1,0:T(8,128)(2,1)} %get-tuple-element.49), channel_id=1, source_target_pairs={{0,4},{1,5},{2,6},{3,7},{4,0},{5,1},{6,2},{7,3},{8,12},{9,13},{10,... | collective-permute-start | bytes 294920 | tf_op jit(solution)/shard_map/ppermute | solution.py:344
  33.4 33.3 %collective-permute-start.13 = (bf16[8,48,128]{2,1,0:T(8,128)(2,1)}, bf16[8,48,128]{2,1,0:T(8,128)(2,1)S(1)}, u32[]{:S(2)}, u32[]{:S(2)}) collective-permute-start(bf16[8,48,128]{2,1,0:T(8,128)(2,1)} %get-tuple-element.50), channel_id=1, source_target_pairs={{0,5},{1,4},{2,7},{3,6},{4,1},{5,0},{6,3},{7,2},{8,13},{9,12},{10,... | collective-permute-start | bytes 294920 | tf_op jit(solution)/shard_map/ppermute | solution.py:344
  58.4 15.6 %collective-permute-start.1 = (bf16[12,48,128]{2,1,0:T(8,128)(2,1)S(1)}, bf16[12,48,128]{2,1,0:T(8,128)(2,1)S(1)}, u32[]{:S(2)}, u32[]{:S(2)}) collective-permute-start(bf16[12,48,128]{2,1,0:T(8,128)(2,1)S(1)} %get-tuple-element.38), channel_id=1, source_target_pairs={{0,1},{1,0},{2,3},{3,2},{4,5},{5,4},{6,7},{7,6},{8,9},{9,8},{10,11... | collective-permute-start | bytes 442376 | tf_op jit(solution)/shard_map/ppermute | solution.py:344
  58.4 18.2 %collective-permute-start.2 = (bf16[12,48,128]{2,1,0:T(8,128)(2,1)S(1)}, bf16[12,48,128]{2,1,0:T(8,128)(2,1)S(1)}, u32[]{:S(2)}, u32[]{:S(2)}) collective-permute-start(bf16[12,48,128]{2,1,0:T(8,128)(2,1)S(1)} %get-tuple-element.39), channel_id=1, source_target_pairs={{0,2},{1,3},{2,0},{3,1},{4,6},{5,7},{6,4},{7,5},{8,10},{9,11},{10,... | collective-permute-start | bytes 442376 | tf_op jit(solution)/shard_map/ppermute | solution.py:344
  71.1 10.5 %collective-permute-start.3 = (bf16[12,48,128]{2,1,0:T(8,128)(2,1)}, bf16[12,48,128]{2,1,0:T(8,128)(2,1)S(1)}, u32[]{:S(2)}, u32[]{:S(2)}) collective-permute-start(bf16[12,48,128]{2,1,0:T(8,128)(2,1)} %get-tuple-element.40), channel_id=1, source_target_pairs={{0,3},{1,2},{2,1},{3,0},{4,7},{5,6},{6,5},{7,4},{8,11},{9,10},{10,... | collective-permute-start | bytes 442376 | tf_op jit(solution)/shard_map/ppermute | solution.py:344
  72.4 13.3 %collective-permute-start.4 = (bf16[12,48,128]{2,1,0:T(8,128)(2,1)}, bf16[12,48,128]{2,1,0:T(8,128)(2,1)S(1)}, u32[]{:S(2)}, u32[]{:S(2)}) collective-permute-start(bf16[12,48,128]{2,1,0:T(8,128)(2,1)} %get-tuple-element.41), channel_id=1, source_target_pairs={{0,4},{1,5},{2,6},{3,7},{4,0},{5,1},{6,2},{7,3},{8,12},{9,13},{10,... | collective-permute-start | bytes 442376 | tf_op jit(solution)/shard_map/ppermute | solution.py:344
  73.7 13.6 %collective-permute-start.5 = (bf16[12,48,128]{2,1,0:T(8,128)(2,1)}, bf16[12,48,128]{2,1,0:T(8,128)(2,1)S(1)}, u32[]{:S(2)}, u32[]{:S(2)}) collective-permute-start(bf16[12,48,128]{2,1,0:T(8,128)(2,1)} %get-tuple-element.42), channel_id=1, source_target_pairs={{0,5},{1,4},{2,7},{3,6},{4,1},{5,0},{6,3},{7,2},{8,13},{9,12},{10,... | collective-permute-start | bytes 442376 | tf_op jit(solution)/shard_map/ppermute | solution.py:344
  74.0 13.3 %collective-permute-start.6 = (bf16[12,48,128]{2,1,0:T(8,128)(2,1)}, bf16[12,48,128]{2,1,0:T(8,128)(2,1)S(1)}, u32[]{:S(2)}, u32[]{:S(2)}) collective-permute-start(bf16[12,48,128]{2,1,0:T(8,128)(2,1)} %get-tuple-element.43), channel_id=1, source_target_pairs={{0,6},{1,7},{2,4},{3,5},{4,2},{5,3},{6,0},{7,1},{8,14},{9,15},{10,... | collective-permute-start | bytes 442376 | tf_op jit(solution)/shard_map/ppermute | solution.py:344
  76.6 10.7 %collective-permute-start.7 = (bf16[12,48,128]{2,1,0:T(8,128)(2,1)}, bf16[12,48,128]{2,1,0:T(8,128)(2,1)S(1)}, u32[]{:S(2)}, u32[]{:S(2)}) collective-permute-start(bf16[12,48,128]{2,1,0:T(8,128)(2,1)} %copy-done.24), channel_id=1, source_target_pairs={{0,7},{1,6},{2,5},{3,4},{4,3},{5,2},{6,1},{7,0},{8,15},{9,14},{10,... | collective-permute-start | bytes 442376 | tf_op jit(solution)/shard_map/ppermute | solution.py:344
  103.2 13.5 %collective-permute-start.23 = (bf16[24,24,128]{2,1,0:T(8,128)(2,1)}, bf16[24,24,128]{2,1,0:T(8,128)(2,1)}, u32[]{:S(2)}, u32[]{:S(2)}) collective-permute-start(bf16[24,24,128]{2,1,0:T(8,128)(2,1)} %get-tuple-element.62), channel_id=1, source_target_pairs={{0,1},{1,0},{2,3},{3,2},{4,5},{5,4},{6,7},{7,6},{8,9},{9,8},{10,11... | collective-permute-start | bytes 442376 | tf_op jit(solution)/shard_map/ppermute | solution.py:344
  103.8 13.9 %collective-permute-start.24 = (bf16[24,24,128]{2,1,0:T(8,128)(2,1)}, bf16[24,24,128]{2,1,0:T(8,128)(2,1)}, u32[]{:S(2)}, u32[]{:S(2)}) collective-permute-start(bf16[24,24,128]{2,1,0:T(8,128)(2,1)} %get-tuple-element.63), channel_id=1, source_target_pairs={{0,2},{1,3},{2,0},{3,1},{4,6},{5,7},{6,4},{7,5},{8,10},{9,11},{10,... | collective-permute-start | bytes 442376 | tf_op jit(solution)/shard_map/ppermute | solution.py:344
  112.2 18.4 %collective-permute-start.25 = (bf16[24,24,128]{2,1,0:T(8,128)(2,1)}, bf16[24,24,128]{2,1,0:T(8,128)(2,1)}, u32[]{:S(2)}, u32[]{:S(2)}) collective-permute-start(bf16[24,24,128]{2,1,0:T(8,128)(2,1)} %copy-done.27), channel_id=1, source_target_pairs={{0,3},{1,2},{2,1},{3,0},{4,7},{5,6},{6,5},{7,4},{8,11},{9,10},{10,... | collective-permute-start | bytes 442376 | tf_op jit(solution)/shard_map/ppermute | solution.py:344
  113.6 17.1 %collective-permute-start.26 = (bf16[24,24,128]{2,1,0:T(8,128)(2,1)}, bf16[24,24,128]{2,1,0:T(8,128)(2,1)}, u32[]{:S(2)}, u32[]{:S(2)}) collective-permute-start(bf16[24,24,128]{2,1,0:T(8,128)(2,1)} %copy-done.26), channel_id=1, source_target_pairs={{0,4},{1,5},{2,6},{3,7},{4,0},{5,1},{6,2},{7,3},{8,12},{9,13},{10,... | collective-permute-start | bytes 442376 | tf_op jit(solution)/shard_map/ppermute | solution.py:344
  116.5 14.8 %collective-permute-start.27 = (bf16[24,24,128]{2,1,0:T(8,128)(2,1)}, bf16[24,24,128]{2,1,0:T(8,128)(2,1)}, u32[]{:S(2)}, u32[]{:S(2)}) collective-permute-start(bf16[24,24,128]{2,1,0:T(8,128)(2,1)} %copy-done.25), channel_id=1, source_target_pairs={{0,5},{1,4},{2,7},{3,6},{4,1},{5,0},{6,3},{7,2},{8,13},{9,12},{10,... | collective-permute-start | bytes 442376 | tf_op jit(solution)/shard_map/ppermute | solution.py:344
  116.6 15.6 %collective-permute-start.28 = (bf16[24,24,128]{2,1,0:T(8,128)(2,1)}, bf16[24,24,128]{2,1,0:T(8,128)(2,1)}, u32[]{:S(2)}, u32[]{:S(2)}) collective-permute-start(bf16[24,24,128]{2,1,0:T(8,128)(2,1)} %copy-done.23), channel_id=1, source_target_pairs={{0,6},{1,7},{2,4},{3,5},{4,2},{5,3},{6,0},{7,1},{8,14},{9,15},{10,... | collective-permute-start | bytes 442376 | tf_op jit(solution)/shard_map/ppermute | solution.py:344
  117.6 16.4 %collective-permute-start.29 = (bf16[24,24,128]{2,1,0:T(8,128)(2,1)}, bf16[24,24,128]{2,1,0:T(8,128)(2,1)}, u32[]{:S(2)}, u32[]{:S(2)}) collective-permute-start(bf16[24,24,128]{2,1,0:T(8,128)(2,1)} %copy-done.22), channel_id=1, source_target_pairs={{0,7},{1,6},{2,5},{3,4},{4,3},{5,2},{6,1},{7,0},{8,15},{9,14},{10,... | collective-permute-start | bytes 442376 | tf_op jit(solution)/shard_map/ppermute | solution.py:344
  130.6 10.8 %collective-permute-start.18 = (bf16[24,16,128]{2,1,0:T(8,128)(2,1)}, bf16[24,16,128]{2,1,0:T(8,128)(2,1)S(1)}, u32[]{:S(2)}, u32[]{:S(2)}) collective-permute-start(bf16[24,16,128]{2,1,0:T(8,128)(2,1)} %copy-done.32), channel_id=1, source_target_pairs={{0,3},{1,2},{2,1},{3,0},{4,7},{5,6},{6,5},{7,4},{8,11},{9,10},{10,... | collective-permute-start | bytes 294920 | tf_op jit(solution)/shard_map/ppermute | solution.py:344
  130.7 10.8 %collective-permute-start.19 = (bf16[24,16,128]{2,1,0:T(8,128)(2,1)}, bf16[24,16,128]{2,1,0:T(8,128)(2,1)S(1)}, u32[]{:S(2)}, u32[]{:S(2)}) collective-permute-start(bf16[24,16,128]{2,1,0:T(8,128)(2,1)} %copy-done.31), channel_id=1, source_target_pairs={{0,4},{1,5},{2,6},{3,7},{4,0},{5,1},{6,2},{7,3},{8,12},{9,13},{10,... | collective-permute-start | bytes 294920 | tf_op jit(solution)/shard_map/ppermute | solution.py:344
  131.2 10.2 %collective-permute-start.20 = (bf16[24,16,128]{2,1,0:T(8,128)(2,1)}, bf16[24,16,128]{2,1,0:T(8,128)(2,1)S(1)}, u32[]{:S(2)}, u32[]{:S(2)}) collective-permute-start(bf16[24,16,128]{2,1,0:T(8,128)(2,1)} %copy-done.30), channel_id=1, source_target_pairs={{0,5},{1,4},{2,7},{3,6},{4,1},{5,0},{6,3},{7,2},{8,13},{9,12},{10,... | collective-permute-start | bytes 294920 | tf_op jit(solution)/shard_map/ppermute | solution.py:344
  132.2 9.3 %collective-permute-start.21 = (bf16[24,16,128]{2,1,0:T(8,128)(2,1)}, bf16[24,16,128]{2,1,0:T(8,128)(2,1)S(1)}, u32[]{:S(2)}, u32[]{:S(2)}) collective-permute-start(bf16[24,16,128]{2,1,0:T(8,128)(2,1)} %copy-done.29), channel_id=1, source_target_pairs={{0,6},{1,7},{2,4},{3,5},{4,2},{5,3},{6,0},{7,1},{8,14},{9,15},{10,... | collective-permute-start | bytes 294920 | tf_op jit(solution)/shard_map/ppermute | solution.py:344
  (55 other events, 213.2 us)
